TPU v7x, 32 devices: a whole 2x2x4 slice. The times are simulated.
32 devices in a mesh: fsdp: 8 (over z, x), context: 2 (over y), tensor: 2 (over core).
Axes of the slice: x: 2, y: 2, z: 4, core: 2. Of those that a mesh axis runs over, the one named last changes fastest.
Arguments:
- tokens: bfloat16 [16, 640, 1024], P('fsdp', 'context'), may hold values from -6 to 6
- segments: int32 [16, 640], P('fsdp'), may hold values from 0 to 1, as said below
- first_gain: float32 [1024], replicated, may hold values from 0.1 to 1.9
- first_shift: float32 [1024], replicated, may hold values from -4 to 4
- input_weight: bfloat16 [1024, 3, 1024], P(('fsdp', 'context'), None, 'tensor'), may hold values from -0.1875 to 0.1875
- input_bias: float32 [2, 1024], P(None, 'tensor'), may hold values from -6 to 6
- output_weight: bfloat16 [1024, 1024], P(('fsdp', 'context'), 'tensor'), may hold values from -2.5 to 2.5
- output_bias: float32 [2, 1024], replicated, may hold values from -6 to 6
- second_gain: float32 [1024], replicated, may hold values from 0.1 to 1.9
- second_shift: float32 [1024], replicated, may hold values from -4 to 4
- up_weight: bfloat16 [1024, 4096], P(('fsdp', 'context'), 'tensor'), may hold values from -0.1875 to 0.1875
- up_bias: float32 [4096], P('tensor'), may hold values from -6 to 6
- down_weight: bfloat16 [1024, 4096], P(('fsdp', 'context'), 'tensor'), may hold values from -0.09375 to 0.09375
- cotangent: bfloat16 [16, 640, 1024], P('fsdp', 'context'), may hold values from -6 to 6
Outputs:
- block_output: bfloat16 [16, 640, 1024], P('fsdp', 'context')
- tokens_gradient: float32 [16, 640, 1024], P('fsdp', 'context')
- first_gain_gradient: float32 [1024], replicated
- first_shift_gradient: float32 [1024], replicated
- input_weight_gradient: float32 [1024, 3, 1024], P(('fsdp', 'context'), None, 'tensor')
- input_bias_gradient: float32 [2, 1024], P(None, 'tensor')
- output_weight_gradient: float32 [1024, 1024], P(('fsdp', 'context'), 'tensor')
- output_bias_gradient: float32 [2, 1024], replicated
- second_gain_gradient: float32 [1024], replicated
- second_shift_gradient: float32 [1024], replicated
- up_weight_gradient: float32 [1024, 4096], P(('fsdp', 'context'), 'tensor')
- up_bias_gradient: float32 [4096], P('tensor')
- down_weight_gradient: float32 [1024, 4096], P(('fsdp', 'context'), 'tensor')
- clipped_weight: float32 [1024, 2, 1024], P(('fsdp', 'context'), None, 'tensor')
- clip_factor: float32 [16], P('tensor')
Inputs may be any that keep to these rules, and one draw needn't show every extreme that they name: `segments`: each row of 640 slots holds one image: 577 consecutive slots with segment number 1, starting at a drawn offset; all other slots are 0.
All inputs are finite; a program needn't handle non-finite values.
Results may differ from a plain program's by a relative error of at most 0.014.
Values may be sent and summed in bfloat16 or wider, within the bound.
A program may use at most 128 MiB of HBM per device.

v0:
```python
import jax
import jax.numpy as jnp
from jax import lax
from jax.sharding import PartitionSpec as P

HEAD_DIM = 64


EPSILON = 1e-06
CLIP_LIMIT = 1.5
MASKED = -1e30
HALF_ROOT = 0.7071067811865476
DENSITY = 0.3989422804014327


def normalize(values, gain, shift):
    average = jnp.mean(values, axis=-1, keepdims=True)
    centered = values - average
    inverse = lax.rsqrt(jnp.mean(centered * centered, axis=-1, keepdims=True) + EPSILON)
    scaled = centered * inverse
    return (scaled * gain + shift, scaled, inverse)


def normalize_back(incoming, scaled, inverse, gain):
    weighted = incoming * gain
    bracket = (
        weighted
        - jnp.mean(weighted, axis=-1, keepdims=True)
        - scaled * jnp.mean(weighted * scaled, axis=-1, keepdims=True)
    )
    return (inverse * bracket, jnp.sum(incoming * scaled, axis=0), jnp.sum(incoming, axis=0))


def gelu_slope(values):
    return (
        0.5 * (1.0 + lax.erf(values * HALF_ROOT))
        + values * jnp.exp(-0.5 * values * values) * DENSITY
    )


def split_heads(values):
    shaped = values.reshape(values.shape[0], values.shape[1], -1, HEAD_DIM)
    return jnp.transpose(shaped, (2, 0, 1, 3))


def join_heads(values):
    moved = jnp.transpose(values, (1, 2, 0, 3))
    return moved.reshape(moved.shape[0], moved.shape[1], -1)


def on_device(
    tokens,
    segments,
    first_gain,
    first_shift,
    input_weight,
    input_bias,
    output_weight,
    output_bias,
    second_gain,
    second_shift,
    up_weight,
    up_bias,
    down_weight,
    cotangent,
):
    group = tokens.shape[0]
    tok_rows = tokens.shape[1]
    width = tokens.shape[2]
    score_scale = HEAD_DIM ** (-0.5)
    position = lax.axis_index("context") * tok_rows
    query_segments = lax.dynamic_slice_in_dim(segments, position, tok_rows, 1)
    allowed = segments[:, None, :] == query_segments[:, :, None]
    real_pairs = allowed & (query_segments[:, :, None] > 0)
    keep_rows = (query_segments > 0).astype(jnp.float32).reshape(-1)[:, None]
    input_full, output_full = (
        lax.all_gather(input_weight, ("fsdp", "context"), axis=0, tiled=True),
        lax.all_gather(output_weight, ("fsdp", "context"), axis=0, tiled=True),
    )
    tokens_float = tokens.astype(jnp.float32).reshape(group * tok_rows, width)
    normed_one, scaled_one, inverse_one = normalize(tokens_float, first_gain, first_shift)
    first_operand = normed_one.astype(jnp.bfloat16)
    projected = jnp.einsum(
        "td,dcf->tcf", first_operand, input_full, preferred_element_type=jnp.float32
    )
    bias_rows = jnp.stack([input_bias[0], jnp.zeros_like(input_bias[0]), input_bias[1]])
    projected = (projected + bias_rows[None]).astype(jnp.bfloat16)
    local_width = projected.shape[2]
    projected = projected.reshape(group, tok_rows, 3, local_width)
    sources = lax.all_gather(projected[:, :, 1:], "context", axis=1, tiled=True)
    query_heads = split_heads(projected[:, :, 0])
    key_heads = split_heads(sources[:, :, 0])
    value_heads = split_heads(sources[:, :, 1])

    def head_forward(operands):
        query_one, key_one, value_one = operands
        logits = (
            jnp.einsum("gqd,gkd->gqk", query_one, key_one, preferred_element_type=jnp.float32)
            * score_scale
        )
        masked = jnp.where(allowed, logits, MASKED)
        summit = jnp.max(jnp.where(real_pairs, logits, MASKED))
        highest = jnp.max(masked, axis=2, keepdims=True)
        powers = jnp.exp(masked - highest)
        totals = jnp.sum(powers, axis=2, keepdims=True)
        weights_low = (powers / totals).astype(jnp.bfloat16)
        mixed = jnp.einsum(
            "gqk,gkd->gqd", weights_low, value_one, preferred_element_type=jnp.float32
        )
        return (mixed.astype(jnp.bfloat16), (highest + jnp.log(totals))[:, :, 0], summit)

    head_context, log_totals, summits = lax.map(head_forward, (query_heads, key_heads, value_heads))
    context = join_heads(head_context).reshape(group * tok_rows, local_width)
    attended = lax.psum(
        jnp.einsum("tf,df->td", context, output_full, preferred_element_type=jnp.float32), "tensor"
    )
    residual = tokens_float + attended + output_bias[0]
    peaks = lax.pmax(summits, ("fsdp", "context"))
    up_full, down_full = (
        lax.all_gather(up_weight, ("fsdp", "context"), axis=0, tiled=True),
        lax.all_gather(down_weight, ("fsdp", "context"), axis=0, tiled=True),
    )
    normed_two, scaled_two, inverse_two = normalize(residual, second_gain, second_shift)
    second_operand = normed_two.astype(jnp.bfloat16)
    pre_act = jnp.dot(second_operand, up_full, preferred_element_type=jnp.float32) + up_bias
    hidden = jax.nn.gelu(pre_act, approximate=False).astype(jnp.bfloat16)
    mixed_sum = lax.psum(
        jnp.einsum("tf,df->td", hidden, down_full, preferred_element_type=jnp.float32).astype(
            jnp.bfloat16
        ),
        "tensor",
    ).astype(jnp.float32)
    block_output = ((residual + mixed_sum + output_bias[1]) * keep_rows).astype(jnp.bfloat16)
    factor = CLIP_LIMIT / jnp.maximum(peaks, CLIP_LIMIT)
    column_scale = jnp.repeat(jnp.sqrt(factor), HEAD_DIM)
    clipped_weight = input_weight[:, :2, :].astype(jnp.float32) * column_scale[None, None, :]
    input_full, output_full, up_full, down_full = (
        lax.all_gather(input_weight, ("fsdp", "context"), axis=0, tiled=True),
        lax.all_gather(output_weight, ("fsdp", "context"), axis=0, tiled=True),
        lax.all_gather(up_weight, ("fsdp", "context"), axis=0, tiled=True),
        lax.all_gather(down_weight, ("fsdp", "context"), axis=0, tiled=True),
    )
    upstream = cotangent.astype(jnp.float32).reshape(group * tok_rows, width) * keep_rows
    upstream_low = upstream.astype(jnp.bfloat16)
    down_gradient = jnp.einsum(
        "td,tf->df", upstream_low, hidden, preferred_element_type=jnp.float32
    )
    pre_gradient = (
        jnp.dot(upstream_low, down_full, preferred_element_type=jnp.float32) * gelu_slope(pre_act)
    ).astype(jnp.bfloat16)
    up_gradient = jnp.einsum(
        "td,tf->df", second_operand, pre_gradient, preferred_element_type=jnp.float32
    )
    up_bias_gradient = jnp.sum(pre_gradient.astype(jnp.float32), axis=0)
    second_gradient = lax.psum(
        jnp.einsum("tf,df->td", pre_gradient, up_full, preferred_element_type=jnp.float32), "tensor"
    )
    through_two, second_gain_gradient, second_shift_gradient = normalize_back(
        second_gradient, scaled_two, inverse_two, second_gain
    )
    residual_gradient = upstream + through_two
    output_bias_gradient = jnp.stack(
        [jnp.sum(residual_gradient, axis=0), jnp.sum(upstream, axis=0)]
    )
    attend_low = residual_gradient.astype(jnp.bfloat16)
    output_gradient = jnp.einsum(
        "td,tf->df", attend_low, context, preferred_element_type=jnp.float32
    )
    context_back = jnp.dot(attend_low, output_full, preferred_element_type=jnp.float32).astype(
        jnp.bfloat16
    )
    context_gradient = split_heads(context_back.reshape(group, tok_rows, local_width))

    def head_backward(operands):
        query_one, key_one, value_one, incoming, log_total = operands
        logits = (
            jnp.einsum("gqd,gkd->gqk", query_one, key_one, preferred_element_type=jnp.float32)
            * score_scale
        )
        probs = jnp.exp(jnp.where(allowed, logits, MASKED) - log_total[:, :, None])
        prob_gradient = jnp.einsum(
            "gqd,gkd->gqk", incoming, value_one, preferred_element_type=jnp.float32
        )
        centre = jnp.sum(probs * prob_gradient, axis=2, keepdims=True)
        score_low = (probs * (prob_gradient - centre) * score_scale).astype(jnp.bfloat16)
        query_gradient = jnp.einsum(
            "gqk,gkd->gqd", score_low, key_one, preferred_element_type=jnp.float32
        ).astype(jnp.bfloat16)
        key_gradient = jnp.einsum(
            "gqk,gqd->gkd", score_low, query_one, preferred_element_type=jnp.float32
        )
        value_gradient = jnp.einsum(
            "gqk,gqd->gkd", probs.astype(jnp.bfloat16), incoming, preferred_element_type=jnp.float32
        )
        return (query_gradient, key_gradient, value_gradient)

    query_grads, key_grads, value_grads = lax.map(
        head_backward, (query_heads, key_heads, value_heads, context_gradient, log_totals)
    )
    source_terms = jnp.stack([join_heads(key_grads), join_heads(value_grads)], axis=2)
    source_sums = lax.psum_scatter(
        source_terms.astype(jnp.bfloat16), "context", scatter_dimension=1, tiled=True
    )
    source_low = source_sums.reshape(group * tok_rows, 2, local_width)
    query_flat = join_heads(query_grads).reshape(group * tok_rows, local_width)
    projected_gradient = jnp.concatenate([query_flat[:, None, :], source_low], axis=1)
    input_gradient = jnp.einsum(
        "td,tcf->dcf", first_operand, projected_gradient, preferred_element_type=jnp.float32
    )
    input_bias_gradient = jnp.stack(
        [
            jnp.sum(projected_gradient[:, 0].astype(jnp.float32), axis=0),
            jnp.sum(projected_gradient[:, 2].astype(jnp.float32), axis=0),
        ]
    )
    first_gradient = lax.psum(
        jnp.einsum(
            "tcf,dcf->td", projected_gradient, input_full, preferred_element_type=jnp.float32
        ).astype(jnp.bfloat16),
        "tensor",
    ).astype(jnp.float32)
    through_one, first_gain_gradient, first_shift_gradient = normalize_back(
        first_gradient, scaled_one, inverse_one, first_gain
    )
    tokens_gradient = (residual_gradient + through_one).reshape(group, tok_rows, width)
    block_output = block_output.reshape(group, tok_rows, width)
    (
        first_gain_sum,
        first_shift_sum,
        input_bias_sum,
        output_bias_sum,
        second_gain_sum,
        second_shift_sum,
        up_bias_sum,
    ) = lax.psum(
        (
            first_gain_gradient,
            first_shift_gradient,
            input_bias_gradient,
            output_bias_gradient,
            second_gain_gradient,
            second_shift_gradient,
            up_bias_gradient,
        ),
        ("fsdp", "context"),
    )
    input_sum, output_sum, up_sum, down_sum = (
        lax.psum_scatter(input_gradient, ("fsdp", "context"), scatter_dimension=0, tiled=True),
        lax.psum_scatter(output_gradient, ("fsdp", "context"), scatter_dimension=0, tiled=True),
        lax.psum_scatter(up_gradient, ("fsdp", "context"), scatter_dimension=0, tiled=True),
        lax.psum_scatter(down_gradient, ("fsdp", "context"), scatter_dimension=0, tiled=True),
    )
    return (
        block_output,
        tokens_gradient,
        first_gain_sum,
        first_shift_sum,
        input_sum,
        input_bias_sum,
        output_sum,
        output_bias_sum,
        second_gain_sum,
        second_shift_sum,
        up_sum,
        up_bias_sum,
        down_sum,
        clipped_weight,
        factor,
    )


def solution(mesh):
    placed = (
        P("fsdp", "context", None),
        P("fsdp", None),
        P(),
        P(),
        P(("fsdp", "context"), None, "tensor"),
        P(None, "tensor"),
        P(("fsdp", "context"), "tensor"),
        P(),
        P(),
        P(),
        P(("fsdp", "context"), "tensor"),
        P("tensor"),
        P(("fsdp", "context"), "tensor"),
        P("fsdp", "context", None),
    )
    return jax.shard_map(
        on_device,
        mesh=mesh,
        in_specs=placed,
        out_specs=(
            P("fsdp", "context", None),
            P("fsdp", "context", None),
            P(),
            P(),
            P(("fsdp", "context"), None, "tensor"),
            P(None, "tensor"),
            P(("fsdp", "context"), "tensor"),
            P(),
            P(),
            P(),
            P(("fsdp", "context"), "tensor"),
            P("tensor"),
            P(("fsdp", "context"), "tensor"),
            P(("fsdp", "context"), None, "tensor"),
            P("tensor"),
        ),
        check_vma=False,
    )
```

profile of v0, /device:TPU:0, one launch (start us, length us, event | category | flops | bytes accessed | tf_op | source)
XLA Modules:
  0.0 1274.7 jit_solution(16076587097010745818)
XLA Ops:
  12.3 69.0 %all-gather.6.cloned.1.call-done = bf16[1024,3,512]{2,0,1:T(8,128)(2,1)} async-done(((bf16[64,3,512]{2,0,1:T(8,128)(2,1)}), bf16[1024,3,512]{2,0,1:T(8,128)(2,1)}) %all-gather.6.cloned.1.call-update) | async-done | bytes 3145744 | tf_op jit(solution)/shard_map/all_gather | solution.py:77
  81.3 4.1 add_convert_fusion
  91.7 35.4 %all-gather.8.cloned.1.call-done = bf16[2,640,2,512]{3,2,0,1:T(2,128)(2,1)} async-done(((bf16[2,320,2,512]{3,2,0,1:T(2,128)(2,1)}), bf16[2,640,2,512]{3,2,0,1:T(2,128)(2,1)}) %all-gather.8.cloned.1.call-update) | async-done | bytes 2621456 | tf_op jit(solution)/shard_map/all_gather | solution.py:90
  127.1 7.7 fusion.117
  134.8 6.1 copy.83
  143.4 4.6 copy.84
  150.7 49.3 %while.32 = (s32[]{:T(128)}, bf16[8,2,320,64]{2,3,1,0:T(8,128)(2,1)S(1)}, f32[8,2,320]{2,1,0:T(2,128)}, f32[8]{0:T(128)S(1)}, bf16[8,2,320,64]{2,3,1,0:T(8,128)(...) while((s32[]{:T(128)}, ...), condition=%wide.region_6.7_spmd.clone.clone, body=%wide.region_2.6_spmd.clone.clone.sunk | while | flops 112270720 | bytes 5488893 | solution.py:112
  202.2 3.6 fusion.120
  208.6 19.7 %all-reduce.8.cloned.1.call-done = f32[640,1024]{1,0:T(8,128)} async-done(((f32[640,1024]{1,0:T(8,128)}), f32[640,1024]{1,0:T(8,128)}) %all-reduce.8.cloned.1.call-update) | async-done | bytes 2621456 | tf_op jit(solution)/shard_map/psum | solution.py:114
  231.2 76.4 %all-gather.12.cloned.1.call-done = bf16[1024,2048]{1,0:T(8,128)(2,1)} async-done(((bf16[64,2048]{1,0:T(8,128)(2,1)}), bf16[1024,2048]{1,0:T(8,128)(2,1)}) %all-gather.12.cloned.1.call-update) | async-done | bytes 4194320 | tf_op jit(solution)/shard_map/all_gather | solution.py:120
  307.6 18.2 %fusion.71 = (bf16[640,2048]{1,0:T(8,128)(2,1)}, f32[640,2048]{1,0:T(8,128)}) fusion(f32[2048]{0:T(1024)S(1)} %copy-done.29, bf16[1024,2048]{1,0:T(8,128)(2,1)} %all-gather.12.cloned.1.call-done, f32[640,1024]{1,0:T(8,128)S(1)} %get-tuple-element.320, f32[1024]{0:T(1024)S(1)} %copy-done.30, f32[1024]{0:T(1024)S(1)} %copy-done.22, ...), kind=kOutput, calls=%fused_computation.68 | convolution fusion | flops 2774138880 | bytes 14701568 | tf_op jit(solution)/shard_map/dot_general | solution.py:125
  325.8 58.6 %all-gather.14.cloned.1.call-done = bf16[1024,2048]{1,0:T(8,128)(2,1)} async-done(((bf16[64,2048]{1,0:T(8,128)(2,1)}), bf16[1024,2048]{1,0:T(8,128)(2,1)}) %all-gather.14.cloned.1.call-update) | async-done | bytes 4194320 | tf_op jit(solution)/shard_map/all_gather | solution.py:121
  384.4 8.1 convert_reduce_fusion
  394.0 4.4 fusion.121
  398.4 10.7 all-reduce.12.cloned.1.call-start
  409.2 10.3 all-reduce.10.cloned.1.call-done
  429.9 138.2 %while.31 = (s32[]{:T(128)}, bf16[8,2,320,64]{2,3,1,0:T(8,128)(2,1)S(1)}, bf16[8,2,640,64]{2,3,0,1:T(8,128)(2,1)}, bf16[8,2,640,64]{2,3,0,1:T(8,128)(2,1)}, bf16...) while((s32[]{:T(128)}, ...), condition=%wide.region_16.17_spmd.clone, body=%wide.region_14.16_spmd.clone.sunk | while | flops 268331520 | bytes 19811452 | solution.py:197
  436.8 4.3 fusion.164
  441.1 3.7 fusion.163
  454.1 4.3 fusion.164
  458.4 3.7 fusion.163
  471.4 4.3 fusion.164
  475.7 3.7 fusion.163
  488.6 4.3 fusion.164
  492.9 3.7 fusion.163
  505.9 4.3 fusion.164
  510.2 3.7 fusion.163
  523.2 4.3 fusion.164
  527.5 3.7 fusion.163
  540.5 4.3 fusion.164
  544.8 3.7 fusion.163
  557.8 4.3 fusion.164
  562.0 3.7 fusion.163
  568.1 3.5 pad_maximum_fusion
  571.6 7.5 copy.67
  581.0 6.9 convolution_convert_fusion.1
  592.4 62.4 %all-reduce.12.cloned.1.call-done = bf16[2,640,2,512]{3,2,0,1:T(2,128)(2,1)} async-done(((bf16[2,640,2,512]{3,2,0,1:T(2,128)(2,1)}), bf16[2,640,2,512]{3,2,0,1:T(2,128)(2,1)}) %all-reduce.12.cloned.1.call-update) | async-done | bytes 2621456
  658.6 3.3 bitcast_convert_fusion
  662.0 4.3 fusion.105
  666.3 7.8 fusion.110
  674.4 9.3 fusion.122
  683.8 7.2 fusion.102
  694.3 41.1 %pmax.7 = f32[8]{0:T(128)S(1)} all-reduce(f32[8]{0:T(128)S(1)} %copy-done.34), channel_id=1, replica_groups=mesh['fsdp'=8,'context'=2,'tensor'=2] {'fsdp','context'}, use_global_device_ids=true, to_apply=%region_41.42 | all-reduce | flops 8 | bytes 64 | tf_op jit(solution)/shard_map/pmax | solution.py:118
  742.3 77.6 %all-reduce.1 = (f32[1024]{0:T(1024)}, f32[1024]{0:T(1024)}, f32[2,512]{1,0:T(2,128)}, f32[2,1024]{1,0:T(2,128)}, f32[1024]{0:T(1024)}, /*index=5*/f32[1024]{0:T(1024)}, f32[2048]{0:T(1024)}) all-reduce(f32[1024]{0:T(1024)S(1)} %get-tuple-element.255, ...), channel_id=1, replica_groups=mesh['fsdp'=8,'context'=2,'tensor'=2] {'fsdp','context'}, use_global_device_ids=true, to_apply=%region_22.23 | all-reduce | flops 9216 | bytes 73728 | tf_op jit(solution)/shard_map/psum | solution.py:235
  819.9 2.9 multiply_convert_fusion.1
  825.5 123.9 %reduce-scatter.9.cloned.1.call-done = f32[64,2048]{1,0:T(8,128)} async-done(((f32[1024,2048]{1,0:T(8,128)}), f32[64,2048]{1,0:T(8,128)}) %reduce-scatter.9.cloned.1.call-update) | async-done | bytes 524304 | tf_op jit(solution)/shard_map/reduce_scatter | solution.py:250
  949.4 180.4 %reduce-scatter.11.cloned.1.call-done = f32[64,2048]{1,0:T(8,128)} async-done(((f32[1024,2048]{1,0:T(8,128)}), f32[64,2048]{1,0:T(8,128)}) %reduce-scatter.11.cloned.1.call-update) | async-done | bytes 524304 | tf_op jit(solution)/shard_map/reduce_scatter | solution.py:251
  1129.8 138.0 %reduce-scatter.5.cloned.1.call-done = f32[64,3,512]{2,0,1:T(8,128)} async-done(((f32[1024,3,512]{2,0,1:T(8,128)}), f32[64,3,512]{2,0,1:T(8,128)}) %reduce-scatter.5.cloned.1.call-update) | async-done | bytes 393232 | tf_op jit(solution)/shard_map/reduce_scatter | solution.py:248
  (239 shorter events, 182.2 us)
Async XLA Ops:
  7.2 4.5 copy-start
  7.2 4.4 copy-start.26
  7.2 4.5 copy-start.20
  7.2 4.5 copy-start.25
  7.2 74.1 %all-gather.6.cloned.1.call-start = ((), (), s32[]{:S(2)}) async-start(), calls=%async_computation.4 | async-start | bytes 3342336 | tf_op jit(solution)/shard_map/all_gather | solution.py:77
  8.0 119.1 %all-gather.8.cloned.1.call-start = ((), (), s32[]{:S(2)}) async-start(), calls=%async_computation.5 | async-start | bytes 3932160 | tf_op jit(solution)/shard_map/all_gather | solution.py:90
  9.7 75.8 %copy-start.16 = (f32[640]{0:T(1024)}, f32[640]{0:T(1024)S(1)}, u32[]{:S(2)}) copy-start(f32[640]{0:T(1024)S(1)} %div.38) | copy-start | bytes 7684
  11.6 73.9 %copy-start.18 = (f32[640]{0:T(1024)}, f32[640]{0:T(1024)S(1)}, u32[]{:S(2)}) copy-start(f32[640]{0:T(1024)S(1)} %rsqrt.20) | copy-start | bytes 7684
  12.3 73.1 %copy-start.11 = (bf16[640,1024]{1,0:T(8,128)(2,1)}, bf16[640,1024]{1,0:T(8,128)(2,1)S(1)}, u32[]{:S(2)}) copy-start(bf16[640,1024]{1,0:T(8,128)(2,1)S(1)} %fusion.99) | copy-start | bytes 3932164
  85.4 1.3 copy-start.10
  86.8 3.3 copy-start.15
  89.3 112.1 %all-gather.10.cloned.1.call-start = ((), (), s32[]{:S(2)}) async-start(), calls=%async_computation.6 | async-start | bytes 1114112 | tf_op jit(solution)/shard_map/all_gather | solution.py:78
  90.0 138.3 %all-reduce.8.cloned.1.call-start = ((), (), s32[]{:S(2)}) async-start(), calls=%async_computation.7 | async-start | bytes 5242880 | tf_op jit(solution)/shard_map/psum | solution.py:114
  199.9 5.8 copy-start.13
  199.9 5.8 copy-start.33
  201.3 0.9 copy-start.7
  205.8 1.3 copy-start.23
  205.8 1.3 copy-start.4
  205.8 101.8 %all-gather.12.cloned.1.call-start = ((), (), s32[]{:S(2)}) async-start(), calls=%async_computation.8 | async-start | bytes 4456448 | tf_op jit(solution)/shard_map/all_gather | solution.py:120
  206.4 178.0 %all-gather.14.cloned.1.call-start = ((), (), s32[]{:S(2)}) async-start(), calls=%async_computation.9 | async-start | bytes 4456448 | tf_op jit(solution)/shard_map/all_gather | solution.py:121
  207.0 212.4 %all-reduce.10.cloned.1.call-start = ((), (), s32[]{:S(2)}) async-start(), calls=%async_computation.10 | async-start | bytes 5242880 | tf_op jit(solution)/shard_map/psum | solution.py:155
  230.8 76.9 %copy-start.22 = (f32[1024]{0:T(1024)S(1)}, f32[1024]{0:T(1024)}, u32[]{:S(2)}) copy-start(f32[1024]{0:T(1024)} %param.26) | copy-start | bytes 12292
  230.8 76.8 %copy-start.29 = (f32[2048]{0:T(1024)S(1)}, f32[2048]{0:T(1024)}, u32[]{:S(2)}) copy-start(f32[2048]{0:T(1024)} %param.29) | copy-start | bytes 24580
  230.8 76.8 %copy-start.30 = (f32[1024]{0:T(1024)S(1)}, f32[1024]{0:T(1024)}, u32[]{:S(2)}) copy-start(f32[1024]{0:T(1024)} %param.27) | copy-start | bytes 12292
  384.4 9.6 copy-start.27
  392.5 1.5 copy-start.35
  398.4 256.4 %all-reduce.12.cloned.1.call-start = ((), (), s32[]{:S(2)}) async-start(), calls=%async_computation.15 | async-start | bytes 5242880
  419.4 2.9 copy-start.5
  419.4 2.9 copy-start.6
  422.4 2.8 copy-start.12
  423.7 1.5 copy-start.2
  579.1 160.2 %all-reduce.14.cloned.1.call-start = ((), (), s32[]{:S(2)}) async-start(), calls=%async_computation.16 | async-start | bytes 5242880 | tf_op jit(solution)/shard_map/psum | solution.py:127
  654.8 3.7 copy-start.14
  654.8 3.7 copy-start.28
  657.5 1.1 copy-start.9
  661.9 4.4 copy-start.31
  661.9 163.6 %reduce-scatter.7.cloned.1.call-start = ((), (), s32[]{:S(2)}) async-start(), calls=%async_computation.12 | async-start | bytes 2228224 | tf_op jit(solution)/shard_map/reduce_scatter | solution.py:249
  666.3 283.1 %reduce-scatter.9.cloned.1.call-start = ((), (), s32[]{:S(2)}) async-start(), calls=%async_computation.13 | async-start | bytes 8912896 | tf_op jit(solution)/shard_map/reduce_scatter | solution.py:250
  674.2 455.6 %reduce-scatter.11.cloned.1.call-start = ((), (), s32[]{:S(2)}) async-start(), calls=%async_computation.14 | async-start | bytes 8912896 | tf_op jit(solution)/shard_map/reduce_scatter | solution.py:251
  683.7 584.0 %reduce-scatter.5.cloned.1.call-start = ((), (), s32[]{:S(2)}) async-start(), calls=%async_computation.11 | async-start | bytes 6684672 | tf_op jit(solution)/shard_map/reduce_scatter | solution.py:248
  691.0 3.3 copy-start.34
  691.0 48.4 %copy-start.17 = (f32[640]{0:T(1024)S(1)}, f32[640]{0:T(1024)}, u32[]{:S(2)}) copy-start(f32[640]{0:T(1024)} %copy-done.16) | copy-start | bytes 7684
  691.0 48.4 %copy-start.19 = (f32[640]{0:T(1024)S(1)}, f32[640]{0:T(1024)}, u32[]{:S(2)}) copy-start(f32[640]{0:T(1024)} %copy-done.18) | copy-start | bytes 7684
  691.0 48.4 %copy-start.21 = (f32[1024]{0:T(1024)S(1)}, f32[1024]{0:T(1024)}, u32[]{:S(2)}) copy-start(f32[1024]{0:T(1024)} %param.20) | copy-start | bytes 12292
  692.6 49.7 %copy-start.24 = (f32[2048]{0:T(1024)S(1)}, f32[2048]{0:T(1024)}, u32[]{:S(2)}) copy-start(f32[2048]{0:T(1024)} %get-tuple-element.331) | copy-start | bytes 24580
  819.9 3.0 copy-start.1
  819.9 3.0 copy-start.3
  819.9 3.2 copy-start.8
  (1 other events, 0.7 us)
Sparse Core Ops, SparseCore 0:
  10.8 70.5 all-gather.5
  89.4 37.6 all-gather.7
  129.9 55.0 all-gather.9
  205.9 22.2 all-reduce.7
  230.8 76.7 all-gather.11
  310.2 74.1 all-gather.13
  398.5 20.8 all-reduce.9
  579.2 75.5 all-reduce.11
  662.0 22.2 all-reduce.13
  687.0 82.4 reduce-scatter.6
  772.4 176.9 reduce-scatter.8
  952.1 177.5 reduce-scatter.10
  1132.6 135.1 reduce-scatter.4
where the time goes:
time: 1290 us; the launch traced here: 1270 us
  waiting for transfers between devices  776 us (60%)
  matrix products  228 us (18%)
  blocking collectives  119 us (9%)
  local copies, waits for them, and re-layouts  75.7 us (6%)
  other arithmetic  48.5 us (4%)
  between operations  15.5 us (1%)
    reduce_scatter x1, waiting for transfers between devices, on_device(): lax.psum_scatter(down_gradient, ('fsdp', 'context'), scatter_dimension=0,...  180 us
    reduce_scatter x1, waiting for transfers between devices, on_device(): lax.psum_scatter(input_gradient, ('fsdp', 'context'), scatter_dimension=0...  138 us
    reduce_scatter x1, waiting for transfers between devices, on_device(): lax.psum_scatter(up_gradient, ('fsdp', 'context'), scatter_dimension=0, t...  124 us
    psum x1, blocking collectives, on_device(): lax.psum((first_gain_gradient, first_shift_gradient, input_bias_gradient,...  77.6 us
    all_gather x1, waiting for transfers between devices, on_device(): lax.all_gather(up_weight, ('fsdp', 'context'), axis=0, tiled=True)  76.4 us
    all_gather x1, waiting for transfers between devices, on_device(): lax.all_gather(input_weight, ('fsdp', 'context'), axis=0, tiled=True)  69 us
    unnamed x14, waiting for transfers between devices  64.7 us
    all_gather x1, waiting for transfers between devices, on_device(): lax.all_gather(down_weight, ('fsdp', 'context'), axis=0, tiled=True)  58.6 us
  transfers between devices with their start and end apart: 13, of which 10 were waited for; matrix products, arithmetic and copies ran while one was open for 12% of the time, Pallas kernels for 0%

commit v1 on v0

--- a/solution.py
+++ b/solution.py
@@ -1,6 +1,10 @@
+import functools
+
 import jax
 import jax.numpy as jnp
 from jax import lax
+from jax.experimental import pallas as pl
+from jax.experimental.pallas import tpu as pltpu
 from jax.sharding import PartitionSpec as P
 
 HEAD_DIM = 64
@@ -46,6 +50,891 @@
 def join_heads(values):
     moved = jnp.transpose(values, (1, 2, 0, 3))
     return moved.reshape(moved.shape[0], moved.shape[1], -1)
+
+
+BF = jnp.bfloat16
+F32 = jnp.float32
+COLS = 512
+TILE = 256
+PIECES = 12
+BIG = 1e30
+MESH_ID = pl.DeviceIdType.MESH
+
+
+def nn(left, right):
+    return jnp.dot(left, right, preferred_element_type=F32)
+
+
+def nt(left, right):
+    return lax.dot_general(left, right, (((1,), (1,)), ((), ())), preferred_element_type=F32)
+
+
+def loop(count, body, start=0):
+    def step(index, carry):
+        body(index)
+        return carry
+
+    lax.fori_loop(start, count, step, 0)
+
+
+def part(index, size):
+    return pl.ds(pl.multiple_of(index * size, size), size)
+
+
+def fold(block):
+    return jnp.sum(block.reshape(-1, 8, block.shape[-1]), axis=0)
+
+
+def layer_kernel(
+    chain,
+    tokens,
+    cotangent,
+    weight_in,
+    weight_out,
+    weight_up,
+    weight_down,
+    first_gain,
+    first_shift,
+    bias_three,
+    output_bias,
+    second_gain,
+    second_shift,
+    up_bias,
+    keep_col,
+    keep_row,
+    block_out,
+    token_grad,
+    in_sum,
+    out_sum,
+    up_sum,
+    down_sum,
+    small_out,
+    peak_out,
+    store,
+    near,
+    mid,
+    far,
+    row_in,
+    row_up,
+    plain,
+    first_t,
+    second_t,
+    up_t,
+    heads,
+    context,
+    context_grad,
+    residual,
+    slope,
+    hidden,
+    send,
+    recv,
+    score,
+    other,
+    prob_low,
+    score_low,
+    flip,
+    turned,
+    gather_acc,
+    log_sums,
+    sums,
+    up_sums,
+    head_sums,
+    small,
+    small_x,
+    small_y,
+    small_z,
+    gather_send,
+    gather_recv,
+    local_sem,
+    scatter_send,
+    scatter_recv,
+    pair_send,
+    pair_recv,
+    row_send,
+    row_recv,
+    small_send,
+    small_recv,
+):
+    place = lax.axis_index("fsdp")
+    y = lax.axis_index("context")
+    t = lax.axis_index("tensor")
+    z = place // 2
+    x = place % 2
+    mine = x * 2 + y
+    at_x = (1 - x) * 2 + y
+    at_y = x * 2 + (1 - y)
+    at_xy = (1 - x) * 2 + (1 - y)
+    half = chain // 2
+    to_x = {"fsdp": z * 2 + (1 - x)}
+    to_y = {"context": 1 - y}
+    to_t = {"tensor": 1 - t}
+
+    def to_z(step):
+        return {"fsdp": ((z + step) % chain) * 2 + x}
+
+    def remote(source, target, send_sem, recv_sem, device):
+        return pltpu.make_async_remote_copy(
+            src_ref=source,
+            dst_ref=target,
+            send_sem=send_sem,
+            recv_sem=recv_sem,
+            device_id=device,
+            device_id_type=MESH_ID,
+        )
+
+    slots = row_in.shape[0]
+    own_slots = slots // 2
+    quarter = own_slots // 2
+    width = row_in.shape[1]
+
+    barrier = pltpu.get_barrier_semaphore()
+    for device in [to_x, to_y, to_t] + [to_z(step) for step in range(1, chain)]:
+        pl.semaphore_signal(barrier, inc=1, device_id=device, device_id_type=MESH_ID)
+    pl.semaphore_wait(barrier, chain + 2)
+
+    shards = (
+        [weight_in.at[:, k * COLS : (k + 1) * COLS] for k in range(3)]
+        + [weight_out]
+        + [weight_up.at[:, k * COLS : (k + 1) * COLS] for k in range(4)]
+        + [weight_down.at[:, k * COLS : (k + 1) * COLS] for k in range(4)]
+    )
+
+    def slot_of(j):
+        return j + 8 * (j // 8)
+
+    def gather_copy(j, kind):
+        buf = store.at[slot_of(j)]
+        sems = (gather_send.at[j, kind], gather_recv.at[j, kind])
+        if kind < 3:
+            block = buf.at[z, mine]
+            return remote(block, block, *sems, to_z(kind + 1))
+        if kind == 3:
+            return remote(buf.at[:, mine], buf.at[:, mine], *sems, to_x)
+        if kind == 4:
+            return remote(buf.at[:, mine], buf.at[:, mine], *sems, to_y)
+        if kind == 5:
+            return remote(buf.at[0:half, at_x], buf.at[0:half, at_x], *sems, to_y)
+        return remote(buf.at[half:, at_y], buf.at[half:, at_y], *sems, to_x)
+
+    for j in range(PIECES):
+        pltpu.make_async_copy(shards[j], store.at[slot_of(j), z, mine], local_sem.at[j]).start()
+
+    def load_done(j):
+        pltpu.make_async_copy(shards[j], store.at[slot_of(j), z, mine], local_sem.at[j]).wait()
+
+    def gather_z(j):
+        for step in range(chain - 1):
+            gather_copy(j, step).start()
+
+    def gather_plane(j):
+        for step in range(chain - 1):
+            gather_copy(j, step).wait()
+        gather_copy(j, 3).start()
+        gather_copy(j, 4).start()
+
+    def gather_corner(j):
+        gather_copy(j, 3).wait()
+        gather_copy(j, 5).start()
+        gather_copy(j, 4).wait()
+        gather_copy(j, 6).start()
+
+    def gather_done(j):
+        gather_copy(j, 5).wait()
+        gather_copy(j, 6).wait()
+
+    last = PIECES - 1
+    last_buf = store.at[slot_of(last)]
+    rows = weight_in.shape[0]
+
+    def plane_first(kind):
+        sems = (gather_send.at[last, kind], gather_recv.at[last, kind])
+        if kind < 3:
+            return remote(last_buf.at[z], last_buf.at[z], *sems, to_z(kind + 1))
+        if kind == 3:
+            return remote(last_buf.at[z, mine], last_buf.at[z, mine], *sems, to_x)
+        if kind == 4:
+            return remote(last_buf.at[z, mine], last_buf.at[z, mine], *sems, to_y)
+        if kind == 5:
+            block = last_buf.at[z, at_x, 0 : rows // 2]
+            return remote(block, block, *sems, to_y)
+        block = last_buf.at[z, at_y, rows // 2 :]
+        return remote(block, block, *sems, to_x)
+
+    def row_copies(source, target, which):
+        mine_half = part(y, own_slots)
+        local = pltpu.make_async_copy(source.at[y], target.at[mine_half], row_send.at[which, 2])
+        place_there = pl.ds(pl.multiple_of(y * own_slots + t * quarter, quarter), quarter)
+        across = remote(
+            source.at[1 - y, part(t, quarter)],
+            target.at[place_there],
+            row_send.at[which, 0],
+            row_recv.at[which, 0],
+            to_y,
+        )
+        place_here = pl.ds(pl.multiple_of((1 - y) * own_slots + t * quarter, quarter), quarter)
+        onward = remote(
+            target.at[place_here], target.at[place_here], row_send.at[which, 1], row_recv.at[which, 1], to_t
+        )
+        return local, across, onward
+
+    def row_back(source, target, which):
+        mine_half = part(y, own_slots)
+        local = pltpu.make_async_copy(source.at[mine_half], target.at[y], row_send.at[which, 2])
+        from_here = pl.ds(pl.multiple_of((1 - y) * own_slots + t * quarter, quarter), quarter)
+        across = remote(
+            source.at[from_here],
+            target.at[y, part(t, quarter)],
+            row_send.at[which, 0],
+            row_recv.at[which, 0],
+            to_y,
+        )
+        block = target.at[1 - y, part(t, quarter)]
+        onward = remote(block, block, row_send.at[which, 1], row_recv.at[which, 1], to_t)
+        return local, across, onward
+
+    token_local, token_across, token_on = row_copies(tokens, row_in, 0)
+    up_local, up_across, up_on = row_copies(cotangent, row_up, 1)
+
+    load_done(0)
+    gather_z(0)
+    token_local.start()
+    token_across.start()
+    load_done(last)
+    plane_first(3).start()
+    plane_first(4).start()
+    for j in range(1, PIECES - 1):
+        load_done(j)
+
+    peak_out[...] = jnp.full(peak_out.shape, MASKED, F32)
+    sums[...] = jnp.zeros(sums.shape, F32)
+
+    def stats(values):
+        average = jnp.mean(values, axis=1, keepdims=True)
+        centered = values - average
+        inverse = lax.rsqrt(jnp.mean(centered * centered, axis=1, keepdims=True) + EPSILON)
+        return centered * inverse, inverse
+
+    norm_rows = 32
+
+    def norm_first(i):
+        at = part(i, norm_rows)
+        scaled, _ = stats(row_in[at, :].astype(F32))
+        plain[at, :] = (scaled * first_gain[...] + first_shift[...]).astype(BF)
+
+    def turn(source, target):
+        def body(j):
+            target[part(j, 128), :] = source[:, part(j, 128)].T
+
+        loop(width // 128, body)
+
+    token_across.wait()
+    token_on.start()
+    token_local.wait()
+    gather_plane(0)
+    gather_z(1)
+    plane_first(3).wait()
+    plane_first(5).start()
+    plane_first(4).wait()
+    plane_first(6).start()
+    token_on.wait()
+    loop(slots // norm_rows, norm_first)
+    gather_plane(1)
+    gather_z(2)
+    gather_corner(0)
+    up_local.start()
+    up_across.start()
+    turn(plain, first_t)
+
+    def tick(j):
+        gather_plane(j)
+        gather_z(j + 1)
+        gather_corner(j - 1)
+        gather_done(j - 2)
+
+    def project(c, which):
+        at = part(c, TILE)
+        tile = store[which, :, :, :, at].reshape(width, TILE)
+        heads[which, c] = (nn(plain[...], tile) + bias_three[which, :, at]).astype(BF)
+
+    def project_step(j):
+        tick(j)
+        loop(2, lambda c: project(c, j - 2))
+
+    loop(5, project_step, 2)
+    up_across.wait()
+    up_on.start()
+    up_local.wait()
+
+    lane = lax.broadcasted_iota(jnp.int32, (slots, 128), 1)
+    chunk = 64
+    n_chunks = slots // chunk
+
+    def head_operands(pair, h):
+        where_pair = part(pair % 2, 128)
+        query = heads[0, pair // 2, :, where_pair].astype(F32) * (HEAD_DIM**-0.5)
+        key = heads[1, pair // 2, :, where_pair].astype(F32)
+        own = (lane < HEAD_DIM) if h == 0 else (lane >= HEAD_DIM)
+        first = HEAD_DIM if h == 0 else 0
+        flag = keep_col[...]
+        query = jnp.where(own, query, jnp.where(lane == first, flag, jnp.where(lane == first + 1, 1.0 - flag, 0.0)))
+        key = jnp.where(
+            lane == first, -BIG * (1.0 - flag), jnp.where(lane == first + 1, -BIG * flag, key)
+        )
+        return query.astype(BF), key.astype(BF), own
+
+    def attend(pair):
+        where_pair = part(pair % 2, 128)
+        turned[...] = heads[2, pair // 2, :, where_pair].T
+        for h in range(2):
+            query, key, _ = head_operands(pair, h)
+            score[...] = nt(key, query)
+
+            def top(i, best):
+                return jnp.maximum(best, jnp.max(score[part(i, chunk), :].reshape(-1, 8, slots), axis=0))
+
+            best = lax.fori_loop(0, n_chunks, top, jnp.full((8, slots), -3e38, F32))
+            highest = jnp.max(best, axis=0, keepdims=True)
+
+            def power(i, total):
+                at = part(i, chunk)
+                powers = jnp.exp(score[at, :] - highest)
+                prob_low[at, :] = powers.astype(BF)
+                return total + fold(powers)
+
+            total = lax.fori_loop(0, n_chunks, power, jnp.zeros((8, slots), F32))
+            total = jnp.sum(total, axis=0, keepdims=True)
+            mixed = nn(turned[h * HEAD_DIM : (h + 1) * HEAD_DIM, :], prob_low[...])
+            flip[h * HEAD_DIM : (h + 1) * HEAD_DIM, :] = mixed / total
+            log_sums[2 * pair + h] = highest + jnp.log(total)
+            summit = jnp.max(jnp.where(keep_row[...] > 0.0, highest, MASKED), axis=1, keepdims=True)
+            spots = lax.broadcasted_iota(jnp.int32, peak_out.shape, 1)
+            peak_out[...] = jnp.where(spots == 2 * pair + h, summit, peak_out[...])
+        context[pair // 2, :, where_pair] = flip[...].T.astype(BF)
+
+    def attend_step(i):
+        tick(5 + i)
+        attend(i)
+
+    loop(4, attend_step)
+
+    def mask_rows(i):
+        at = part(i, 64)
+        row_up[at, :] = (row_up[at, :].astype(F32) * keep_col[at, :]).astype(BF)
+
+    up_on.wait()
+    loop(slots // 64, mask_rows)
+    turn(row_up, up_t)
+
+    def pair_copy(slot, j):
+        return remote(send.at[j], recv.at[slot, j], pair_send.at[j], pair_recv.at[slot, j], to_t)
+
+    def pair_sum(slot, product):
+        def body(j):
+            send[j] = product(j).astype(BF)
+            pair_copy(slot, j).start()
+
+        loop(4, body)
+        for j in range(4):
+            pair_copy(slot, j).wait()
+
+    def summed(slot, at):
+        return jnp.concatenate(
+            [send[j, at, :].astype(F32) + recv[slot, j, at, :].astype(F32) for j in range(4)], axis=1
+        )
+
+    def weight_rows(piece, j, c):
+        return store[piece, j, :, :, c * TILE : (c + 1) * TILE].reshape(TILE, TILE)
+
+    def attended(j):
+        return nt(context[0], weight_rows(3, j, 0)) + nt(context[1], weight_rows(3, j, 1))
+
+    tick(9)
+    pair_sum(0, attended)
+
+    def norm_second(i):
+        at = part(i, norm_rows)
+        values = row_in[at, :].astype(F32) + summed(0, at) + output_bias[0:1, :]
+        residual[at, :] = values
+        scaled, _ = stats(values)
+        plain[at, :] = (scaled * second_gain[...] + second_shift[...]).astype(BF)
+
+    loop(slots // norm_rows, norm_second)
+
+    gather_plane(10)
+    for kind in (5, 6):
+        plane_first(kind).wait()
+    for kind in range(chain - 1):
+        plane_first(kind).start()
+    gather_corner(9)
+    gather_done(8)
+
+    def activate(c):
+        at = part(c % 2, TILE)
+        tile = store[4 + c // 2, :, :, :, at].reshape(width, TILE)
+        score[:, 0:TILE] = nn(plain[...], tile) + up_bias[c]
+
+        def rows_of(i):
+            spot = part(i, 64)
+            pre = score[spot, 0:TILE]
+            chance = 0.5 * (1.0 + lax.erf(pre * HALF_ROOT))
+            hidden[c, spot, :] = (pre * chance).astype(BF)
+            slope[c, spot, :] = (chance + pre * jnp.exp(-0.5 * pre * pre) * DENSITY).astype(BF)
+
+        loop(slots // 64, rows_of)
+
+    loop(4, activate)
+    gather_corner(10)
+    gather_done(9)
+    loop(8, activate, 4)
+    turn(plain, second_t)
+
+    def scatter_copy(p, kind):
+        buf = store.at[8 + p]
+        sems = (scatter_send.at[p, kind], scatter_recv.at[p, kind])
+        if kind == 0:
+            return remote(buf.at[0:half, at_xy], near.at[p, 0], *sems, to_y)
+        if kind == 1:
+            return remote(buf.at[half:, at_xy], near.at[p, 1], *sems, to_x)
+        if kind == 2:
+            return remote(buf.at[:, at_x], mid.at[p, 0], *sems, to_x)
+        if kind == 3:
+            return remote(buf.at[:, at_y], mid.at[p, 1], *sems, to_y)
+        step = kind - 3
+        return remote(buf.at[(z + step) % chain, mine], far.at[p, step - 1], *sems, to_z(step))
+
+    def scatter_corner(p):
+        scatter_copy(p, 0).start()
+        scatter_copy(p, 1).start()
+
+    def added(left, right):
+        return (left.astype(F32) + right.astype(F32)).astype(BF)
+
+    def scatter_plane(p):
+        scatter_copy(p, 0).wait()
+        for k in range(half):
+            store[8 + p, k, at_x] = added(store[8 + p, k, at_x], near[p, 0, k])
+        scatter_copy(p, 1).wait()
+        for k in range(half):
+            store[8 + p, half + k, at_y] = added(store[8 + p, half + k, at_y], near[p, 1, k])
+        scatter_copy(p, 2).start()
+        scatter_copy(p, 3).start()
+
+    def scatter_z(p):
+        scatter_copy(p, 2).wait()
+        scatter_copy(p, 3).wait()
+        for k in range(chain):
+            store[8 + p, k, mine] = (
+                store[8 + p, k, mine].astype(F32) + mid[p, 0, k].astype(F32) + mid[p, 1, k].astype(F32)
+            ).astype(BF)
+        for step in range(1, chain):
+            scatter_copy(p, 3 + step).start()
+
+    def scatter_done(p, target, at):
+        for step in range(1, chain):
+            scatter_copy(p, 3 + step).wait()
+        total = store[8 + p, z, mine].astype(F32)
+        for step in range(1, chain):
+            total = total + far[p, step - 1].astype(F32)
+        target[:, at] = total
+
+    def finish(p):
+        if p < 4:
+            scatter_done(p, down_sum, slice(p * COLS, (p + 1) * COLS))
+        elif p < 8:
+            scatter_done(p, up_sum, slice((p - 4) * COLS, (p - 3) * COLS))
+        elif p == 8:
+            scatter_done(p, out_sum, slice(0, COLS))
+        else:
+            scatter_done(p, in_sum, slice((p - 9) * COLS, (p - 8) * COLS))
+
+    def scatter_tick(k):
+        if k < PIECES:
+            scatter_plane(k)
+        if 0 <= k - 1 < PIECES:
+            scatter_z(k - 1)
+        if 0 <= k - 2 < PIECES:
+            finish(k - 2)
+
+    def gradient(left, right, piece, c):
+        def body(m):
+            block = nn(left[part(m, width // 2), :], right)
+            store[8 + piece, part(m, half), :, :, part(c, TILE)] = block.astype(BF).reshape(half, 4, rows, TILE)
+
+        loop(2, body)
+
+    def down_piece(p):
+        loop(2, lambda c: gradient(up_t, hidden[2 * p + c], p, c))
+        scatter_corner(p)
+
+    loop(4, down_piece)
+    gather_done(10)
+    for kind in range(chain - 1):
+        plane_first(kind).wait()
+
+    def back_hidden(c):
+        at = part(c % 2, TILE)
+        tile = store[16 + c // 2, :, :, :, at].reshape(width, TILE)
+        score[:, 0:TILE] = nn(row_up[...], tile)
+
+        def rows_of(i, total):
+            spot = part(i, 64)
+            grad = (score[spot, 0:TILE] * slope[c, spot, :].astype(F32)).astype(BF)
+            slope[c, spot, :] = grad
+            return total + fold(grad.astype(F32))
+
+        total = lax.fori_loop(0, slots // 64, rows_of, jnp.zeros((8, TILE), F32))
+        up_sums[c] = jnp.sum(total, axis=0, keepdims=True)
+
+    loop(8, back_hidden)
+    scatter_tick(0)
+
+    def up_piece(p):
+        loop(2, lambda c: gradient(second_t, slope[2 * p + c], 4 + p, c))
+        scatter_corner(4 + p)
+
+    loop(2, up_piece)
+    scatter_tick(1)
+    loop(4, up_piece, 2)
+    scatter_tick(2)
+
+    def mixed(j):
+        total = nt(hidden[0], weight_rows(16, j, 0))
+        for c in range(1, 8):
+            total = total + nt(hidden[c], weight_rows(16 + c // 2, j, c % 2))
+        return total
+
+    pair_sum(1, mixed)
+
+    def output_rows(i):
+        at = part(i, norm_rows)
+        values = residual[at, :] + summed(1, at) + output_bias[1:2, :]
+        plain[at, :] = (values * keep_col[at, :]).astype(BF)
+
+    loop(slots // norm_rows, output_rows)
+    block_local, block_across, block_on = row_back(plain, block_out, 2)
+    block_local.start()
+    block_across.start()
+    scatter_tick(3)
+
+    def second_back(j):
+        total = nt(slope[0], weight_rows(4, j, 0))
+        for c in range(1, 8):
+            total = total + nt(slope[c], weight_rows(4 + c // 2, j, c % 2))
+        return total
+
+    pair_sum(0, second_back)
+
+    def norm_second_back(i):
+        at = part(i, norm_rows)
+        scaled, inverse = stats(residual[at, :])
+        incoming = summed(0, at)
+        weighted = incoming * second_gain[...]
+        upstream = row_up[at, :].astype(F32)
+        bracket = (
+            weighted
+            - jnp.mean(weighted, axis=1, keepdims=True)
+            - scaled * jnp.mean(weighted * scaled, axis=1, keepdims=True)
+        )
+        total = upstream + inverse * bracket
+        residual[at, :] = total
+        low = total.astype(BF)
+        for j in range(4):
+            hidden[4 + j, at, :] = low[:, j * TILE : (j + 1) * TILE]
+        sums[0] += fold(incoming * scaled)
+        sums[1] += fold(incoming)
+        sums[2] += fold(total)
+        sums[3] += fold(upstream)
+
+    loop(slots // norm_rows, norm_second_back)
+    for j in range(4):
+        for k in range(2):
+            at = j * TILE + k * 128
+            up_t[at : at + 128, :] = hidden[4 + j, :, k * 128 : (k + 1) * 128].T
+    scatter_tick(4)
+    loop(2, lambda c: gradient(up_t, context[c], 8, c))
+    scatter_corner(8)
+
+    def back_context(c):
+        total = None
+        for j in range(4):
+            tile = store[3, j, :, :, part(c, TILE)].reshape(TILE, TILE)
+            term = nn(hidden[4 + j], tile)
+            total = term if total is None else total + term
+        context_grad[c] = total.astype(BF)
+
+    loop(2, back_context)
+    block_across.wait()
+    block_on.start()
+
+    def attend_back(pair):
+        where_pair = part(pair % 2, 128)
+        turned[...] = heads[1, pair // 2, :, where_pair].T
+        value = heads[2, pair // 2, :, where_pair]
+        incoming = context_grad[pair // 2, :, where_pair]
+        for h in range(2):
+            query, key, own = head_operands(pair, h)
+            own_in = jnp.where(own, incoming.astype(F32), 0.0).astype(BF)
+            score[...] = nt(key, query)
+            other[...] = nt(value, own_in)
+            logs = log_sums[2 * pair + h]
+
+            def power(i, total):
+                at = part(i, chunk)
+                probs = jnp.exp(score[at, :] - logs)
+                score[at, :] = probs
+                prob_low[at, :] = probs.astype(BF)
+                return total + fold(probs * other[at, :])
+
+            total = lax.fori_loop(0, n_chunks, power, jnp.zeros((8, slots), F32))
+            centre = jnp.sum(total, axis=0, keepdims=True)
+
+            def rest(i):
+                at = part(i, chunk)
+                score_low[at, :] = (score[at, :] * (other[at, :] - centre)).astype(BF)
+
+            loop(n_chunks, rest)
+            value_grad = nn(prob_low[...], own_in)
+            key_grad = nn(score_low[...], query)
+            if h == 0:
+                gather_acc[0] = value_grad
+                gather_acc[1] = key_grad
+            else:
+                gather_acc[0] += value_grad
+                gather_acc[1] = jnp.where(own, key_grad, gather_acc[1])
+            flip[h * HEAD_DIM : (h + 1) * HEAD_DIM, :] = nn(
+                turned[h * HEAD_DIM : (h + 1) * HEAD_DIM, :], score_low[...]
+            ) * (HEAD_DIM**-0.5)
+        query_low = flip[...].T.astype(BF)
+        value_low = gather_acc[0].astype(BF)
+        heads[0, pair // 2, :, where_pair] = query_low
+        heads[1, pair // 2, :, where_pair] = gather_acc[1].astype(BF)
+        heads[2, pair // 2, :, where_pair] = value_low
+        head_sums[0, pair] = jnp.sum(query_low.astype(F32), axis=0, keepdims=True)
+        head_sums[1, pair] = jnp.sum(value_low.astype(F32), axis=0, keepdims=True)
+
+    for pair in range(4):
+        attend_back(pair)
+        scatter_tick(5 + pair)
+
+    def in_piece(i):
+        loop(2, lambda c: gradient(first_t, heads[i, c], 9 + i, c))
+        scatter_corner(9 + i)
+
+    loop(3, in_piece)
+
+    def first_back(j):
+        total = None
+        for i in range(3):
+            for c in range(2):
+                term = nt(heads[i, c], weight_rows(i, j, c))
+                total = term if total is None else total + term
+        return total
+
+    pair_sum(1, first_back)
+    scatter_tick(9)
+
+    def norm_first_back(i):
+        at = part(i, norm_rows)
+        scaled, inverse = stats(row_in[at, :].astype(F32))
+        incoming = summed(1, at)
+        weighted = incoming * first_gain[...]
+        bracket = (
+            weighted
+            - jnp.mean(weighted, axis=1, keepdims=True)
+            - scaled * jnp.mean(weighted * scaled, axis=1, keepdims=True)
+        )
+        row_in[at, :] = (residual[at, :] + inverse * bracket).astype(BF)
+        sums[4] += fold(incoming * scaled)
+        sums[5] += fold(incoming)
+
+    loop(slots // norm_rows, norm_first_back)
+    grad_local, grad_across, grad_on = row_back(row_in, token_grad, 3)
+    grad_local.start()
+    grad_across.start()
+
+    def collapse(k):
+        return jnp.sum(sums[k], axis=0, keepdims=True)
+
+    small[0:1, :] = collapse(4)
+    small[1:2, :] = collapse(5)
+    small[2:3, :] = jnp.concatenate([head_sums[i, k] for i in range(2) for k in range(4)], axis=1)
+    small[3:4, :] = collapse(2)
+    small[4:5, :] = collapse(3)
+    small[5:6, :] = collapse(0)
+    small[6:7, :] = collapse(1)
+    small[7:8, :] = jnp.concatenate([up_sums[k] for k in range(4)], axis=1)
+    small[8:9, :] = jnp.concatenate([up_sums[4 + k] for k in range(4)], axis=1)
+    small[9:10, :] = jnp.concatenate([peak_out[0:1, :]] * 8, axis=1)
+    small[10:16, :] = jnp.zeros((6, small.shape[1]), F32)
+    row_index = lax.broadcasted_iota(jnp.int32, small.shape, 0)
+
+    def joined(left, right):
+        return jnp.where(row_index == 9, jnp.maximum(left, right), left + right)
+
+    def small_copy(source, target, k, device):
+        return remote(source, target, small_send.at[k], small_recv.at[k], device)
+
+    over_x = small_copy(small, small_x.at[0], 0, to_x)
+    over_x.start()
+    scatter_tick(10)
+    over_x.wait()
+    small_x[1] = joined(small[...], small_x[0])
+    over_y = small_copy(small_x.at[1], small_y, 1, to_y)
+    over_y.start()
+    grad_across.wait()
+    grad_on.start()
+    scatter_tick(11)
+    over_y.wait()
+    small_z[z] = joined(small_x[1], small_y[...])
+    over_z = [small_copy(small_z.at[z], small_z.at[z], 1 + step, to_z(step)) for step in range(1, chain)]
+    for copy in over_z:
+        copy.start()
+    scatter_tick(12)
+    for copy in over_z:
+        copy.wait()
+    total = small_z[0]
+    for k in range(1, chain):
+        total = joined(total, small_z[k])
+    small_out[...] = total
+    scatter_tick(13)
+    block_local.wait()
+    block_on.wait()
+    grad_local.wait()
+    grad_on.wait()
+
+
+def on_device_fused(
+    tokens,
+    segments,
+    first_gain,
+    first_shift,
+    input_weight,
+    input_bias,
+    output_weight,
+    output_bias,
+    second_gain,
+    second_shift,
+    up_weight,
+    up_bias,
+    down_weight,
+    cotangent,
+    chain,
+):
+    group, tok_rows, width = tokens.shape
+    slots = segments.shape[1]
+    rows = input_weight.shape[0]
+    flags = lax.dynamic_slice_in_dim(segments, lax.axis_index("context"), 1, 0).astype(F32)
+    bias_three = jnp.stack([input_bias[0], jnp.zeros_like(input_bias[0]), input_bias[1]])[:, None, :]
+    operands = (
+        tokens,
+        cotangent,
+        input_weight.reshape(rows, -1),
+        output_weight,
+        up_weight,
+        down_weight,
+        first_gain[None],
+        first_shift[None],
+        bias_three,
+        output_bias,
+        second_gain[None],
+        second_shift[None],
+        up_bias.reshape(8, 1, TILE),
+        flags.reshape(slots, 1),
+        flags,
+    )
+    anywhere = pl.BlockSpec(memory_space=pl.ANY)
+    vmem = pl.BlockSpec(memory_space=pltpu.VMEM)
+    half = chain // 2
+    block = (rows, COLS)
+    dma = pltpu.SemaphoreType.DMA
+    results = pl.pallas_call(
+        functools.partial(layer_kernel, chain),
+        out_shape=(
+            jax.ShapeDtypeStruct(tokens.shape, BF),
+            jax.ShapeDtypeStruct(tokens.shape, BF),
+            jax.ShapeDtypeStruct((rows, 3 * COLS), F32),
+            jax.ShapeDtypeStruct((rows, COLS), F32),
+            jax.ShapeDtypeStruct((rows, 4 * COLS), F32),
+            jax.ShapeDtypeStruct((rows, 4 * COLS), F32),
+            jax.ShapeDtypeStruct((16, width), F32),
+            jax.ShapeDtypeStruct((8, 128), F32),
+        ),
+        in_specs=[anywhere] * 6 + [vmem] * 9,
+        out_specs=[anywhere] * 2 + [vmem] * 6,
+        scratch_shapes=[
+            pltpu.VMEM((20, chain, 4) + block, BF),
+            pltpu.VMEM((PIECES, 2, half) + block, BF),
+            pltpu.VMEM((PIECES, 2, chain) + block, BF),
+            pltpu.VMEM((PIECES, chain - 1) + block, BF),
+            pltpu.VMEM((slots, width), BF),
+            pltpu.VMEM((slots, width), BF),
+            pltpu.VMEM((slots, width), BF),
+            pltpu.VMEM((width, slots), BF),
+            pltpu.VMEM((width, slots), BF),
+            pltpu.VMEM((width, slots), BF),
+            pltpu.VMEM((3, 2, slots, TILE), BF),
+            pltpu.VMEM((2, slots, TILE), BF),
+            pltpu.VMEM((2, slots, TILE), BF),
+            pltpu.VMEM((slots, width), F32),
+            pltpu.VMEM((8, slots, TILE), BF),
+            pltpu.VMEM((8, slots, TILE), BF),
+            pltpu.VMEM((4, slots, TILE), BF),
+            pltpu.VMEM((2, 4, slots, TILE), BF),
+            pltpu.VMEM((slots, slots), F32),
+            pltpu.VMEM((slots, slots), F32),
+            pltpu.VMEM((slots, slots), BF),
+            pltpu.VMEM((slots, slots), BF),
+            pltpu.VMEM((128, slots), F32),
+            pltpu.VMEM((128, slots), BF),
+            pltpu.VMEM((2, slots, 128), F32),
+            pltpu.VMEM((8, 1, slots), F32),
+            pltpu.VMEM((6, 8, width), F32),
+            pltpu.VMEM((8, 1, TILE), F32),
+            pltpu.VMEM((2, 4, 1, 128), F32),
+            pltpu.VMEM((16, width), F32),
+            pltpu.VMEM((2, 16, width), F32),
+            pltpu.VMEM((16, width), F32),
+            pltpu.VMEM((chain, 16, width), F32),
+            dma((PIECES, 7)),
+            dma((PIECES, 7)),
+            dma((PIECES,)),
+            dma((PIECES, 7)),
+            dma((PIECES, 7)),
+            dma((4,)),
+            dma((2, 4)),
+            dma((4, 3)),
+            dma((4, 2)),
+            dma((2 + chain,)),
+            dma((2 + chain,)),
+        ],
+        compiler_params=pltpu.CompilerParams(
+            collective_id=0, has_side_effects=True, vmem_limit_bytes=67043328
+        ),
+        name="layer",
+    )(*operands)
+    block_output, tokens_gradient, in_sum, out_sum, up_sum, down_sum, small, _ = results
+    count = input_weight.shape[2] // HEAD_DIM
+    factor = CLIP_LIMIT / jnp.maximum(small[9, :count], CLIP_LIMIT)
+    column_scale = jnp.repeat(jnp.sqrt(factor), HEAD_DIM)
+    clipped_weight = input_weight[:, :2, :].astype(F32) * column_scale[None, None, :]
+    local_width = input_weight.shape[2]
+    return (
+        block_output,
+        tokens_gradient.astype(F32),
+        small[0],
+        small[1],
+        in_sum.reshape(rows, 3, local_width),
+        small[2].reshape(2, local_width),
+        out_sum,
+        small[3:5],
+        small[5],
+        small[6],
+        up_sum,
+        small[7:9].reshape(-1),
+        down_sum,
+        clipped_weight,
+        factor,
+    )
 
 
 def on_device(
@@ -286,8 +1175,12 @@
         P(("fsdp", "context"), "tensor"),
         P("fsdp", "context", None),
     )
+    chain = mesh.shape["fsdp"] // 2
+    step = on_device
+    if mesh.shape["context"] == 2 and mesh.shape["tensor"] == 2 and chain == 4:
+        step = functools.partial(on_device_fused, chain=chain)
     return jax.shard_map(
-        on_device,
+        step,
         mesh=mesh,
         in_specs=placed,
         out_specs=(

time: 1290 us -> 280 us (0.22); the launches traced: 1270 us -> 279 us
  waiting for transfers between devices: 776 us -> 0 us
  Pallas kernels: 0 us -> 261 us
  matrix products: 228 us -> 0 us
  blocking collectives: 119 us -> 0 us
  local copies, waits for them, and re-layouts: 75.7 us -> 10.8 us
  other arithmetic: 48.5 us -> 6.56 us
  between operations: 15.5 us -> 0.7 us
    reduce_scatter x4 -> x0, waiting for transfers between devices: 442 us -> none  [the longest x1 180 us: on_device(): lax.psum_scatter(down_gradient, ('fsdp', 'context'), scatter_dimension=0,...]
    pallas_call x0 -> x1, Pallas kernels: none -> 261 us  [on_device_fused(): pl.pallas_call(functools.partial(layer_kernel, chain), out_shape=(jax.Sha...]
    all_gather x5 -> x0, waiting for transfers between devices: 239 us -> none  [the longest x1 76.4 us: on_device(): lax.all_gather(up_weight, ('fsdp', 'context'), axis=0, tiled=True)]
    dot_general x68 -> x0, matrix products: 228 us -> none  [the longest x8 34.4 us: head_backward(): jnp.einsum('gqk,gqd->gkd', score_low, query_one, preferred_element_type=j...]
    psum x1 -> x0, blocking collectives: 77.6 us -> none  [on_device(): lax.psum((first_gain_gradient, first_shift_gradient, input_bias_gradient,...]
    unnamed x14 -> x0, waiting for transfers between devices: 64.7 us -> none
    pmax x1 -> x0, blocking collectives: 41.1 us -> none  [on_device(): peaks = lax.pmax(summits, ('fsdp', 'context'))]
    psum x3 -> x0, waiting for transfers between devices: 30 us -> none  [the longest x1 19.7 us: on_device(): lax.psum(jnp.einsum('tf,df->td', context, output_full, preferred_element_...]
  transfers between devices with their start and end apart: 13 -> 0, of which waited for: 10 -> 0; matrix products, arithmetic and copies ran while one was open for 12% -> 0% of each run, Pallas kernels for 0% -> 0%
where the time goes in v1:
time: 280 us; the launch traced here: 279 us
  Pallas kernels  261 us (93%)
  local copies, waits for them, and re-layouts  10.8 us (4%)
  other arithmetic  6.56 us (2%)
    pallas_call x1, Pallas kernels, on_device_fused(): pl.pallas_call(functools.partial(layer_kernel, chain), out_shape=(jax.Sha...  261 us

profile of v1, /device:TPU:0, one launch (start us, length us, event | category | flops | bytes accessed | tf_op | source)
XLA Modules:
  0.0 279.3 jit_solution(1563550590712725276)
XLA Ops:
  0.6 1.6 copy.37
  2.3 0.8 fusion.2
  3.0 0.1 pad.1.clone
  3.1 0.1 pad_maximum_fusion
  3.2 0.6 broadcast_in_dim.20.bias_three
  3.8 0.7 fusion.3
  4.5 0.9 copy.33.keep_col
  5.4 1.3 dynamic-slice_convert_fusion.keep_row
  6.7 261.2 %layer.1 = (bf16[2,320,1024]{2,1,0:T(8,128)(2,1)}, bf16[2,320,1024]{2,1,0:T(8,128)(2,1)}, f32[64,1536]{1,0:T(8,128)}, f32[64,512]{1,0:T(8,128)}, f32[64,2048]{1,...) custom-call(bf16[2,320,1024]{2,1,0:T(8,128)(2,1)} %tokens.1, ...), custom_call_target="tpu_custom_call" | custom-call | tf_op jit(solution)/shard_map/layer/pallas_call | solution.py:850
  267.9 0.0 copy-start.6
  267.9 0.0 copy-start.4
  267.9 0.0 copy-start.1
  267.9 3.2 %convert_element_type.10 = f32[2,320,1024]{2,1,0:T(8,128)} convert(bf16[2,320,1024]{2,1,0:T(8,128)(2,1)} %get-tuple-element.23) | non-fusion elementwise | flops 655360 | bytes 3932160 | tf_op jit(solution)/shard_map/convert_element_type | solution.py:923
  271.1 0.0 copy-start
  271.1 0.0 copy-done.6
  271.1 0.6 fusion.1
  271.8 0.0 copy-done.4
  271.8 0.8 copy.41
  272.5 0.6 reshape_squeeze.3
  273.1 0.6 slice_bitcast_fusion
  273.7 0.6 copy.42
  274.3 0.0 copy-done.1
  274.3 0.2 copy.32
  274.5 0.5 fusion
  275.0 0.1 broadcast_in_dim.23
  275.1 0.1 mul.10
  275.2 0.8 convert_multiply_fusion
  276.0 0.0 copy-done
  276.0 0.0 copy-start.5
  276.0 0.0 copy-start.3
  276.0 1.1 copy.47
  277.1 0.0 copy-done.5
  277.1 0.0 copy-start.2
  277.1 0.7 copy.48
  277.7 0.0 copy-done.3
  277.7 0.8 copy.49
  278.5 0.0 copy-done.2
  278.5 0.8 copy.50
Async XLA Ops:
  267.9 3.2 %copy-start.6 = (f32[16,1024]{1,0:T(8,128)S(1)}, f32[16,1024]{1,0:T(8,128)}, u32[]{:S(2)}) copy-start(f32[16,1024]{1,0:T(8,128)} %get-tuple-element.24) | copy-start | bytes 196612
  267.9 3.8 %copy-start.4 = (f32[64,1536]{1,0:T(8,128)S(1)}, f32[64,1536]{1,0:T(8,128)}, u32[]{:S(2)}) copy-start(f32[64,1536]{1,0:T(8,128)} %get-tuple-element.25) | copy-start | bytes 1179652
  267.9 6.4 %copy-start.1 = (bf16[64,3,512]{2,0,1:T(8,128)(2,1)S(1)}, bf16[64,3,512]{2,0,1:T(8,128)(2,1)}, u32[]{:S(2)}) copy-start(bf16[64,3,512]{2,0,1:T(8,128)(2,1)} %param.18) | copy-start | bytes 589828
  271.1 4.9 %copy-start = (bf16[2,320,1024]{2,1,0:T(8,128)(2,1)S(1)}, bf16[2,320,1024]{2,1,0:T(8,128)(2,1)}, u32[]{:S(2)}) copy-start(bf16[2,320,1024]{2,1,0:T(8,128)(2,1)} %get-tuple-element.85) | copy-start | bytes 3932164
  276.0 1.1 copy-start.5
  276.0 1.7 copy-start.3
  277.1 1.5 copy-start.2

commit v2 on v1

--- a/solution.py
+++ b/solution.py
@@ -59,6 +59,269 @@
 PIECES = 12
 BIG = 1e30
 MESH_ID = pl.DeviceIdType.MESH
+GATHER_PIECES = (
+    (0, 0, 256),
+    (0, 256, 256),
+    (1, 0, 512),
+    (2, 0, 512),
+    (3, 0, 512),
+    (4, 0, 512),
+    (5, 0, 512),
+    (6, 0, 512),
+    (7, 0, 512),
+    (8, 0, 512),
+    (9, 0, 512),
+    (10, 0, 512),
+    (11, 0, 512),
+)
+SCATTER_PIECES = (
+    (0, 0, 512),
+    (1, 0, 512),
+    (2, 0, 512),
+    (3, 0, 512),
+    (4, 0, 512),
+    (5, 0, 512),
+    (6, 0, 512),
+    (7, 0, 512),
+    (8, 0, 512),
+    (9, 0, 512),
+    (10, 0, 256),
+    (10, 256, 256),
+    (11, 0, 256),
+    (11, 256, 256),
+)
+GATHER_KINDS = (0, 1, 0, 0, 1, 1, 0, 0, 1, 0, 0, 1, 1)
+SCATTER_KINDS = (1, 1, 1, 0, 1, 1, 0, 1, 1, 0, 0, 0, 0, 0)
+GATHER_SWAPPED = (0, 0, 0, 1, 0, 0, 0, 0, 0, 0, 0, 0, 0)
+SCATTER_SWAPPED = (0, 0, 0, 0, 0, 0, 1, 0, 0, 0, 1, 0, 0, 0)
+GATHER, SCATTER, ROWS, SMALL, COMPUTE = range(5)
+TOKENS, COTANGENT, BLOCK, GRADIENT = range(4)
+(
+    NORM_ONE,
+    TURN_ONE,
+    PROJECT,
+    ATTEND,
+    SEND_ONE,
+    NORM_TWO,
+    TURN_TWO,
+    ACTIVATE,
+    MASK,
+    GRAD_DOWN,
+    BACK_HIDDEN,
+    GRAD_UP,
+    SEND_TWO,
+    OUTPUT,
+    SEND_THREE,
+    BACK_TWO,
+    TURN_BACK,
+    GRAD_OUT,
+    BACK_CONTEXT,
+    ATTEND_BACK,
+    GRAD_IN,
+    SEND_FOUR,
+    BACK_ONE,
+) = range(23)
+SCHEDULE = (
+    (GATHER, 0, 0),
+    (GATHER, 3, 0),
+    (ROWS, TOKENS, 0),
+    (GATHER, 7, 0),
+    (GATHER, 0, 1),
+    (GATHER, 0, 2),
+    (GATHER, 3, 1),
+    (GATHER, 3, 2),
+    (GATHER, 2, 0),
+    (GATHER, 7, 1),
+    (GATHER, 6, 0),
+    (GATHER, 1, 0),
+    (GATHER, 8, 0),
+    (GATHER, 7, 2),
+    (ROWS, TOKENS, 1),
+    (ROWS, TOKENS, 2),
+    (COMPUTE, NORM_ONE, 0),
+    (GATHER, 3, 3),
+    (ROWS, COTANGENT, 0),
+    (GATHER, 1, 1),
+    (GATHER, 7, 3),
+    (GATHER, 2, 1),
+    (GATHER, 2, 2),
+    (COMPUTE, TURN_ONE, 0),
+    (GATHER, 0, 3),
+    (GATHER, 8, 1),
+    (GATHER, 9, 0),
+    (GATHER, 1, 2),
+    (GATHER, 1, 3),
+    (GATHER, 2, 3),
+    (GATHER, 8, 2),
+    (GATHER, 8, 3),
+    (GATHER, 4, 0),
+    (GATHER, 4, 1),
+    (GATHER, 3, 4),
+    (GATHER, 0, 4),
+    (GATHER, 7, 4),
+    (GATHER, 9, 1),
+    (GATHER, 9, 2),
+    (GATHER, 10, 0),
+    (COMPUTE, PROJECT, 2),
+    (ROWS, COTANGENT, 1),
+    (ROWS, COTANGENT, 2),
+    (COMPUTE, MASK, 0),
+    (GATHER, 2, 4),
+    (COMPUTE, PROJECT, 1),
+    (GATHER, 5, 0),
+    (GATHER, 4, 2),
+    (GATHER, 4, 3),
+    (GATHER, 10, 1),
+    (GATHER, 10, 2),
+    (GATHER, 9, 3),
+    (GATHER, 6, 1),
+    (GATHER, 6, 2),
+    (GATHER, 11, 0),
+    (GATHER, 5, 1),
+    (GATHER, 12, 0),
+    (GATHER, 1, 4),
+    (COMPUTE, PROJECT, 0),
+    (COMPUTE, ATTEND, 0),
+    (COMPUTE, ATTEND, 1),
+    (COMPUTE, ATTEND, 2),
+    (COMPUTE, ATTEND, 3),
+    (GATHER, 5, 2),
+    (GATHER, 5, 3),
+    (GATHER, 11, 1),
+    (GATHER, 6, 3),
+    (GATHER, 12, 1),
+    (GATHER, 4, 4),
+    (COMPUTE, SEND_ONE, 0),
+    (COMPUTE, NORM_TWO, 0),
+    (COMPUTE, ACTIVATE, 2),
+    (COMPUTE, GRAD_DOWN, 2),
+    (SCATTER, 2, 0),
+    (COMPUTE, TURN_TWO, 0),
+    (GATHER, 5, 4),
+    (COMPUTE, ACTIVATE, 0),
+    (COMPUTE, GRAD_DOWN, 0),
+    (SCATTER, 0, 0),
+    (GATHER, 10, 3),
+    (GATHER, 11, 2),
+    (GATHER, 11, 3),
+    (GATHER, 8, 4),
+    (COMPUTE, ACTIVATE, 3),
+    (COMPUTE, GRAD_DOWN, 3),
+    (GATHER, 12, 2),
+    (GATHER, 12, 3),
+    (SCATTER, 2, 1),
+    (GATHER, 9, 4),
+    (COMPUTE, BACK_HIDDEN, 0),
+    (COMPUTE, GRAD_UP, 0),
+    (SCATTER, 4, 0),
+    (GATHER, 6, 4),
+    (COMPUTE, ACTIVATE, 1),
+    (COMPUTE, GRAD_DOWN, 1),
+    (SCATTER, 1, 0),
+    (GATHER, 10, 4),
+    (COMPUTE, BACK_HIDDEN, 1),
+    (COMPUTE, GRAD_UP, 1),
+    (SCATTER, 5, 0),
+    (GATHER, 11, 4),
+    (COMPUTE, BACK_HIDDEN, 2),
+    (COMPUTE, GRAD_UP, 2),
+    (SCATTER, 6, 0),
+    (SCATTER, 0, 1),
+    (GATHER, 12, 4),
+    (COMPUTE, SEND_TWO, 0),
+    (COMPUTE, BACK_HIDDEN, 3),
+    (COMPUTE, GRAD_UP, 3),
+    (SCATTER, 7, 0),
+    (COMPUTE, OUTPUT, 0),
+    (COMPUTE, SEND_THREE, 0),
+    (ROWS, BLOCK, 0),
+    (SCATTER, 3, 0),
+    (SCATTER, 1, 1),
+    (SCATTER, 2, 2),
+    (SCATTER, 4, 1),
+    (SCATTER, 0, 2),
+    (COMPUTE, BACK_TWO, 0),
+    (COMPUTE, BACK_CONTEXT, 0),
+    (COMPUTE, ATTEND_BACK, 2),
+    (COMPUTE, ATTEND_BACK, 1),
+    (COMPUTE, TURN_BACK, 0),
+    (SCATTER, 7, 1),
+    (SCATTER, 6, 1),
+    (COMPUTE, GRAD_OUT, 0),
+    (SCATTER, 8, 0),
+    (SCATTER, 1, 2),
+    (SCATTER, 3, 1),
+    (SCATTER, 5, 1),
+    (SCATTER, 4, 2),
+    (COMPUTE, ATTEND_BACK, 3),
+    (COMPUTE, ATTEND_BACK, 0),
+    (COMPUTE, GRAD_IN, 3),
+    (SCATTER, 11, 0),
+    (COMPUTE, SEND_FOUR, 0),
+    (COMPUTE, GRAD_IN, 1),
+    (COMPUTE, GRAD_IN, 5),
+    (SCATTER, 13, 0),
+    (SCATTER, 7, 2),
+    (SCATTER, 8, 1),
+    (SCATTER, 3, 2),
+    (COMPUTE, GRAD_IN, 4),
+    (SCATTER, 12, 0),
+    (SCATTER, 6, 2),
+    (SCATTER, 11, 1),
+    (COMPUTE, GRAD_IN, 0),
+    (SCATTER, 9, 0),
+    (SCATTER, 5, 2),
+    (COMPUTE, BACK_ONE, 0),
+    (ROWS, GRADIENT, 0),
+    (SMALL, 0, 0),
+    (SMALL, 0, 1),
+    (SCATTER, 8, 2),
+    (SCATTER, 12, 1),
+    (SCATTER, 9, 1),
+    (COMPUTE, GRAD_IN, 2),
+    (SCATTER, 10, 0),
+    (SCATTER, 3, 3),
+    (SCATTER, 13, 1),
+    (SCATTER, 0, 3),
+    (ROWS, BLOCK, 1),
+    (SCATTER, 5, 3),
+    (SCATTER, 11, 2),
+    (SCATTER, 11, 3),
+    (SMALL, 0, 2),
+    (ROWS, GRADIENT, 1),
+    (ROWS, GRADIENT, 2),
+    (SCATTER, 7, 3),
+    (SCATTER, 2, 3),
+    (SCATTER, 12, 2),
+    (SCATTER, 12, 3),
+    (SCATTER, 9, 2),
+    (SCATTER, 10, 1),
+    (SCATTER, 6, 3),
+    (SCATTER, 8, 3),
+    (SCATTER, 8, 4),
+    (SCATTER, 10, 2),
+    (SCATTER, 1, 3),
+    (SCATTER, 4, 3),
+    (SCATTER, 13, 2),
+    (SCATTER, 0, 4),
+    (SCATTER, 10, 3),
+    (SCATTER, 2, 4),
+    (SMALL, 0, 3),
+    (SCATTER, 3, 4),
+    (SCATTER, 13, 3),
+    (ROWS, BLOCK, 2),
+    (SCATTER, 9, 3),
+    (SCATTER, 1, 4),
+    (SCATTER, 4, 4),
+    (SCATTER, 7, 4),
+    (SCATTER, 12, 4),
+    (SCATTER, 5, 4),
+    (SCATTER, 11, 4),
+    (SCATTER, 10, 4),
+    (SCATTER, 13, 4),
+    (SCATTER, 6, 4),
+    (SCATTER, 9, 4),
+)
 
 
 def nn(left, right):
@@ -89,19 +352,18 @@
     chain,
     tokens,
     cotangent,
+    segments,
     weight_in,
     weight_out,
     weight_up,
     weight_down,
     first_gain,
     first_shift,
-    bias_three,
+    input_bias,
     output_bias,
     second_gain,
     second_shift,
     up_bias,
-    keep_col,
-    keep_row,
     block_out,
     token_grad,
     in_sum,
@@ -109,11 +371,9 @@
     up_sum,
     down_sum,
     small_out,
-    peak_out,
     store,
-    near,
-    mid,
-    far,
+    over_b,
+    over_rest,
     row_in,
     row_up,
     plain,
@@ -131,7 +391,6 @@
     score,
     other,
     prob_low,
-    score_low,
     flip,
     turned,
     gather_acc,
@@ -143,6 +402,10 @@
     small_x,
     small_y,
     small_z,
+    keep_col,
+    keep_row,
+    peaks,
+    block_sum,
     gather_send,
     gather_recv,
     local_sem,
@@ -160,17 +423,35 @@
     t = lax.axis_index("tensor")
     z = place // 2
     x = place % 2
+    half = chain // 2
     mine = x * 2 + y
-    at_x = (1 - x) * 2 + y
-    at_y = x * 2 + (1 - y)
-    at_xy = (1 - x) * 2 + (1 - y)
-    half = chain // 2
+    at_ab = (1 - x) * 2 + (1 - y)
     to_x = {"fsdp": z * 2 + (1 - x)}
     to_y = {"context": 1 - y}
     to_t = {"tensor": 1 - t}
 
-    def to_z(step):
-        return {"fsdp": ((z + step) % chain) * 2 + x}
+    def sides(swapped):
+        if swapped:
+            return x * 2 + (1 - y), (1 - x) * 2 + y, to_y, to_x
+        a_x = x + (1 - t) * (1 - 2 * x)
+        a_y = y + t * (1 - 2 * y)
+        b_x = x + t * (1 - 2 * x)
+        b_y = y + (1 - t) * (1 - 2 * y)
+        to_a = {"fsdp": z * 2 + a_x, "context": a_y}
+        to_b = {"fsdp": z * 2 + b_x, "context": b_y}
+        return a_x * 2 + a_y, b_x * 2 + b_y, to_a, to_b
+
+    normal_sides = sides(0)
+    swapped_sides = sides(1)
+
+    near = 1 - z + 4 * (z // 2)
+    mate = 3 - z
+    far = 3 - near
+    inner = ((z + 1) // 2) % 2 == 1
+    outer = ((z + 1) // 2) % 2 == 0
+
+    def to_z(k):
+        return {"fsdp": k * 2 + x}
 
     def remote(source, target, send_sem, recv_sem, device):
         return pltpu.make_async_remote_copy(
@@ -187,78 +468,116 @@
     quarter = own_slots // 2
     width = row_in.shape[1]
 
-    barrier = pltpu.get_barrier_semaphore()
-    for device in [to_x, to_y, to_t] + [to_z(step) for step in range(1, chain)]:
-        pl.semaphore_signal(barrier, inc=1, device_id=device, device_id_type=MESH_ID)
-    pl.semaphore_wait(barrier, chain + 2)
-
     shards = (
-        [weight_in.at[:, k * COLS : (k + 1) * COLS] for k in range(3)]
+        [weight_in.at[k] for k in range(3)]
         + [weight_out]
         + [weight_up.at[:, k * COLS : (k + 1) * COLS] for k in range(4)]
         + [weight_down.at[:, k * COLS : (k + 1) * COLS] for k in range(4)]
     )
-
-    def slot_of(j):
-        return j + 8 * (j // 8)
-
-    def gather_copy(j, kind):
-        buf = store.at[slot_of(j)]
-        sems = (gather_send.at[j, kind], gather_recv.at[j, kind])
-        if kind < 3:
-            block = buf.at[z, mine]
-            return remote(block, block, *sems, to_z(kind + 1))
-        if kind == 3:
-            return remote(buf.at[:, mine], buf.at[:, mine], *sems, to_x)
-        if kind == 4:
-            return remote(buf.at[:, mine], buf.at[:, mine], *sems, to_y)
-        if kind == 5:
-            return remote(buf.at[0:half, at_x], buf.at[0:half, at_x], *sems, to_y)
-        return remote(buf.at[half:, at_y], buf.at[half:, at_y], *sems, to_x)
+    rows = weight_out.shape[0]
+
+    def load(j):
+        return pltpu.make_async_copy(shards[j], store.at[j + 8 * (j // 8), z, mine], local_sem.at[j])
 
     for j in range(PIECES):
-        pltpu.make_async_copy(shards[j], store.at[slot_of(j), z, mine], local_sem.at[j]).start()
-
-    def load_done(j):
-        pltpu.make_async_copy(shards[j], store.at[slot_of(j), z, mine], local_sem.at[j]).wait()
-
-    def gather_z(j):
-        for step in range(chain - 1):
-            gather_copy(j, step).start()
-
-    def gather_plane(j):
-        for step in range(chain - 1):
-            gather_copy(j, step).wait()
-        gather_copy(j, 3).start()
-        gather_copy(j, 4).start()
-
-    def gather_corner(j):
-        gather_copy(j, 3).wait()
-        gather_copy(j, 5).start()
-        gather_copy(j, 4).wait()
-        gather_copy(j, 6).start()
-
-    def gather_done(j):
-        gather_copy(j, 5).wait()
-        gather_copy(j, 6).wait()
-
-    last = PIECES - 1
-    last_buf = store.at[slot_of(last)]
-    rows = weight_in.shape[0]
-
-    def plane_first(kind):
-        sems = (gather_send.at[last, kind], gather_recv.at[last, kind])
-        if kind < 3:
-            return remote(last_buf.at[z], last_buf.at[z], *sems, to_z(kind + 1))
-        if kind == 3:
-            return remote(last_buf.at[z, mine], last_buf.at[z, mine], *sems, to_x)
-        if kind == 4:
-            return remote(last_buf.at[z, mine], last_buf.at[z, mine], *sems, to_y)
-        if kind == 5:
-            block = last_buf.at[z, at_x, 0 : rows // 2]
-            return remote(block, block, *sems, to_y)
-        block = last_buf.at[z, at_y, rows // 2 :]
-        return remote(block, block, *sems, to_x)
+        load(j).start()
+
+    barrier = pltpu.get_barrier_semaphore()
+    for device in [to_x, to_y, to_t] + [to_z((z + step) % chain) for step in range(1, chain)]:
+        pl.semaphore_signal(barrier, inc=1, device_id=device, device_id_type=MESH_ID)
+    pl.semaphore_wait(barrier, chain + 2)
+
+    def gathered(j, at, quarter_at):
+        piece, start, count = GATHER_PIECES[j]
+        return store.at[piece + 8 * (piece // 8), at, quarter_at, :, start : start + count]
+
+    def gather_way(j):
+        return swapped_sides if GATHER_SWAPPED[j] else normal_sides
+
+    def gather_z(j, stream, source, slot, target):
+        block = gathered(j, source, gather_way(j)[0] if stream else mine)
+        return remote(
+            block,
+            block,
+            gather_send.at[j, 4 * stream + slot],
+            gather_recv.at[j, 4 * stream + source],
+            to_z(target),
+        )
+
+    def gather_start(j, stream):
+        gather_z(j, stream, z, 0, near).start()
+        gather_z(j, stream, z, 1, mate).start()
+
+        @pl.when(outer)
+        def _():
+            gather_z(j, stream, z, 2, far).start()
+
+    def gather_pass(j, stream):
+        @pl.when(inner)
+        def _():
+            gather_z(j, stream, mate, 0, z).wait_recv()
+            gather_z(j, stream, mate, 3, near).start()
+
+    def gather_end(j, stream):
+        gather_z(j, stream, near, 0, z).wait_recv()
+        gather_z(j, stream, far, 0, z).wait_recv()
+        gather_z(j, stream, z, 0, near).wait_send()
+        gather_z(j, stream, z, 1, mate).wait_send()
+
+        @pl.when(outer)
+        def _():
+            gather_z(j, stream, mate, 0, z).wait_recv()
+            gather_z(j, stream, z, 2, far).wait_send()
+
+        @pl.when(inner)
+        def _():
+            gather_z(j, stream, z, 3, near).wait_send()
+
+    def gather_side(j, kind):
+        at_a, _, to_a, to_b = gather_way(j)
+        everything = slice(None)
+        if kind == 0:
+            block, device = gathered(j, z if GATHER_KINDS[j] else everything, mine), to_a
+        elif kind == 1:
+            block, device = gathered(j, everything, mine), to_b
+        else:
+            block, device = gathered(j, everything, at_a), to_b
+        return remote(block, block, gather_send.at[j, 8 + kind], gather_recv.at[j, 8 + kind], device)
+
+    def gather_stage(j, stage):
+        piece = GATHER_PIECES[j][0]
+        if piece not in loaded:
+            load(piece).wait()
+            loaded.add(piece)
+        if stage == 4:
+            gather_side(j, 1).wait()
+            gather_side(j, 2).wait()
+        elif GATHER_KINDS[j]:
+            if stage == 0:
+                gather_side(j, 0).start()
+                gather_start(j, 0)
+            elif stage == 1:
+                gather_side(j, 0).wait()
+                gather_start(j, 1)
+                gather_pass(j, 0)
+            elif stage == 2:
+                gather_pass(j, 1)
+            else:
+                gather_end(j, 0)
+                gather_side(j, 1).start()
+                gather_end(j, 1)
+                gather_side(j, 2).start()
+        elif stage == 0:
+            gather_start(j, 0)
+        elif stage == 1:
+            gather_pass(j, 0)
+        elif stage == 2:
+            gather_end(j, 0)
+            gather_side(j, 0).start()
+            gather_side(j, 1).start()
+        else:
+            gather_side(j, 0).wait()
+            gather_side(j, 2).start()
 
     def row_copies(source, target, which):
         mine_half = part(y, own_slots)
@@ -295,18 +614,7 @@
     token_local, token_across, token_on = row_copies(tokens, row_in, 0)
     up_local, up_across, up_on = row_copies(cotangent, row_up, 1)
 
-    load_done(0)
-    gather_z(0)
-    token_local.start()
-    token_across.start()
-    load_done(last)
-    plane_first(3).start()
-    plane_first(4).start()
-    for j in range(1, PIECES - 1):
-        load_done(j)
-
-    peak_out[...] = jnp.full(peak_out.shape, MASKED, F32)
-    sums[...] = jnp.zeros(sums.shape, F32)
+    loaded = set()
 
     def stats(values):
         average = jnp.mean(values, axis=1, keepdims=True)
@@ -316,6 +624,12 @@
 
     norm_rows = 32
 
+    def prepare():
+        peaks[...] = jnp.full(peaks.shape, MASKED, F32)
+        sums[...] = jnp.zeros(sums.shape, F32)
+        keep_row[...] = jnp.where(segments[pl.ds(y, 1), :] > 0, 1.0, 0.0)
+        keep_col[...] = jnp.broadcast_to(keep_row[...], (128, slots)).T
+
     def norm_first(i):
         at = part(i, norm_rows)
         scaled, _ = stats(row_in[at, :].astype(F32))
@@ -327,43 +641,13 @@
 
         loop(width // 128, body)
 
-    token_across.wait()
-    token_on.start()
-    token_local.wait()
-    gather_plane(0)
-    gather_z(1)
-    plane_first(3).wait()
-    plane_first(5).start()
-    plane_first(4).wait()
-    plane_first(6).start()
-    token_on.wait()
-    loop(slots // norm_rows, norm_first)
-    gather_plane(1)
-    gather_z(2)
-    gather_corner(0)
-    up_local.start()
-    up_across.start()
-    turn(plain, first_t)
-
-    def tick(j):
-        gather_plane(j)
-        gather_z(j + 1)
-        gather_corner(j - 1)
-        gather_done(j - 2)
-
     def project(c, which):
         at = part(c, TILE)
         tile = store[which, :, :, :, at].reshape(width, TILE)
-        heads[which, c] = (nn(plain[...], tile) + bias_three[which, :, at]).astype(BF)
-
-    def project_step(j):
-        tick(j)
-        loop(2, lambda c: project(c, j - 2))
-
-    loop(5, project_step, 2)
-    up_across.wait()
-    up_on.start()
-    up_local.wait()
+        value = nn(plain[...], tile)
+        if which != 1:
+            value = value + input_bias[which // 2 : which // 2 + 1, at]
+        heads[which, c] = value.astype(BF)
 
     lane = lax.broadcasted_iota(jnp.int32, (slots, 128), 1)
     chunk = 64
@@ -375,7 +659,7 @@
         key = heads[1, pair // 2, :, where_pair].astype(F32)
         own = (lane < HEAD_DIM) if h == 0 else (lane >= HEAD_DIM)
         first = HEAD_DIM if h == 0 else 0
-        flag = keep_col[...]
+        flag = keep_col[:, 0:1]
         query = jnp.where(own, query, jnp.where(lane == first, flag, jnp.where(lane == first + 1, 1.0 - flag, 0.0)))
         key = jnp.where(
             lane == first, -BIG * (1.0 - flag), jnp.where(lane == first + 1, -BIG * flag, key)
@@ -407,23 +691,13 @@
             flip[h * HEAD_DIM : (h + 1) * HEAD_DIM, :] = mixed / total
             log_sums[2 * pair + h] = highest + jnp.log(total)
             summit = jnp.max(jnp.where(keep_row[...] > 0.0, highest, MASKED), axis=1, keepdims=True)
-            spots = lax.broadcasted_iota(jnp.int32, peak_out.shape, 1)
-            peak_out[...] = jnp.where(spots == 2 * pair + h, summit, peak_out[...])
+            spots = lax.broadcasted_iota(jnp.int32, peaks.shape, 1)
+            peaks[...] = jnp.where(spots == 2 * pair + h, summit, peaks[...])
         context[pair // 2, :, where_pair] = flip[...].T.astype(BF)
-
-    def attend_step(i):
-        tick(5 + i)
-        attend(i)
-
-    loop(4, attend_step)
 
     def mask_rows(i):
         at = part(i, 64)
-        row_up[at, :] = (row_up[at, :].astype(F32) * keep_col[at, :]).astype(BF)
-
-    up_on.wait()
-    loop(slots // 64, mask_rows)
-    turn(row_up, up_t)
+        row_up[at, :] = (row_up[at, :].astype(F32) * keep_col[at, 0:1]).astype(BF)
 
     def pair_copy(slot, j):
         return remote(send.at[j], recv.at[slot, j], pair_send.at[j], pair_recv.at[slot, j], to_t)
@@ -434,6 +708,8 @@
             pair_copy(slot, j).start()
 
         loop(4, body)
+
+    def pair_wait(slot):
         for j in range(4):
             pair_copy(slot, j).wait()
 
@@ -447,9 +723,6 @@
 
     def attended(j):
         return nt(context[0], weight_rows(3, j, 0)) + nt(context[1], weight_rows(3, j, 1))
-
-    tick(9)
-    pair_sum(0, attended)
 
     def norm_second(i):
         at = part(i, norm_rows)
@@ -458,20 +731,10 @@
         scaled, _ = stats(values)
         plain[at, :] = (scaled * second_gain[...] + second_shift[...]).astype(BF)
 
-    loop(slots // norm_rows, norm_second)
-
-    gather_plane(10)
-    for kind in (5, 6):
-        plane_first(kind).wait()
-    for kind in range(chain - 1):
-        plane_first(kind).start()
-    gather_corner(9)
-    gather_done(8)
-
     def activate(c):
         at = part(c % 2, TILE)
         tile = store[4 + c // 2, :, :, :, at].reshape(width, TILE)
-        score[:, 0:TILE] = nn(plain[...], tile) + up_bias[c]
+        score[:, 0:TILE] = nn(plain[...], tile) + up_bias[0:1, part(c, TILE)]
 
         def rows_of(i):
             spot = part(i, 64)
@@ -482,78 +745,144 @@
 
         loop(slots // 64, rows_of)
 
-    loop(4, activate)
-    gather_corner(10)
-    gather_done(9)
-    loop(8, activate, 4)
-    turn(plain, second_t)
-
-    def scatter_copy(p, kind):
-        buf = store.at[8 + p]
+    def z_spot(p, stream, spot):
+        return (stream if SCATTER_KINDS[p] else 1) * chain + spot
+
+    def columns(p):
+        _, start, count = SCATTER_PIECES[p]
+        return slice(start, start + count)
+
+    def scatter_way(p):
+        return swapped_sides if SCATTER_SWAPPED[p] else normal_sides
+
+    def partial(p, at, quarter_at):
+        return store.at[8 + SCATTER_PIECES[p][0], at, quarter_at, :, columns(p)]
+
+    def from_b(p, which, at):
+        return over_b.at[SCATTER_PIECES[p][0], which, at, :, columns(p)]
+
+    def from_rest(p, at):
+        return over_rest.at[SCATTER_PIECES[p][0], at, :, columns(p)]
+
+    def scatter_side(p, kind):
+        at_a, at_b, to_a, to_b = scatter_way(p)
         sems = (scatter_send.at[p, kind], scatter_recv.at[p, kind])
+        everything = slice(None)
         if kind == 0:
-            return remote(buf.at[0:half, at_xy], near.at[p, 0], *sems, to_y)
+            return remote(partial(p, everything, at_b), from_b(p, 0, everything), *sems, to_b)
         if kind == 1:
-            return remote(buf.at[half:, at_xy], near.at[p, 1], *sems, to_x)
-        if kind == 2:
-            return remote(buf.at[:, at_x], mid.at[p, 0], *sems, to_x)
-        if kind == 3:
-            return remote(buf.at[:, at_y], mid.at[p, 1], *sems, to_y)
-        step = kind - 3
-        return remote(buf.at[(z + step) % chain, mine], far.at[p, step - 1], *sems, to_z(step))
-
-    def scatter_corner(p):
-        scatter_copy(p, 0).start()
-        scatter_copy(p, 1).start()
-
-    def added(left, right):
-        return (left.astype(F32) + right.astype(F32)).astype(BF)
-
-    def scatter_plane(p):
-        scatter_copy(p, 0).wait()
-        for k in range(half):
-            store[8 + p, k, at_x] = added(store[8 + p, k, at_x], near[p, 0, k])
-        scatter_copy(p, 1).wait()
-        for k in range(half):
-            store[8 + p, half + k, at_y] = added(store[8 + p, half + k, at_y], near[p, 1, k])
-        scatter_copy(p, 2).start()
-        scatter_copy(p, 3).start()
-
-    def scatter_z(p):
-        scatter_copy(p, 2).wait()
-        scatter_copy(p, 3).wait()
-        for k in range(chain):
-            store[8 + p, k, mine] = (
-                store[8 + p, k, mine].astype(F32) + mid[p, 0, k].astype(F32) + mid[p, 1, k].astype(F32)
-            ).astype(BF)
-        for step in range(1, chain):
-            scatter_copy(p, 3 + step).start()
-
-    def scatter_done(p, target, at):
-        for step in range(1, chain):
-            scatter_copy(p, 3 + step).wait()
-        total = store[8 + p, z, mine].astype(F32)
-        for step in range(1, chain):
-            total = total + far[p, step - 1].astype(F32)
-        target[:, at] = total
-
-    def finish(p):
-        if p < 4:
-            scatter_done(p, down_sum, slice(p * COLS, (p + 1) * COLS))
-        elif p < 8:
-            scatter_done(p, up_sum, slice((p - 4) * COLS, (p - 3) * COLS))
-        elif p == 8:
-            scatter_done(p, out_sum, slice(0, COLS))
+            return remote(partial(p, everything, at_ab), from_b(p, 1, everything), *sems, to_b)
+        if SCATTER_KINDS[p]:
+            return remote(partial(p, z, at_a), from_rest(p, 2 * chain), *sems, to_a)
+        return remote(partial(p, everything, at_a), from_rest(p, slice(0, chain)), *sems, to_a)
+
+    def own_quarter(p, stream):
+        return scatter_way(p)[0] if stream else mine
+
+    def scatter_z(p, stream, slot, block, spot, target):
+        return remote(
+            partial(p, block, own_quarter(p, stream)),
+            from_rest(p, z_spot(p, stream, spot)),
+            scatter_send.at[p, 3 + 4 * stream + slot],
+            scatter_recv.at[p, 3 + 4 * stream + spot],
+            to_z(target),
+        )
+
+    def add_to(ref, *terms):
+        total = ref[...].astype(F32)
+        for term in terms:
+            total = total + term[...].astype(F32)
+        ref[...] = total.astype(BF)
+
+    def scatter_start(p, stream):
+        scatter_z(p, stream, 0, near, z, near).start()
+
+        @pl.when(outer)
+        def _():
+            scatter_z(p, stream, 1, mate, z, mate).start()
+            scatter_z(p, stream, 2, far, near, near).start()
+
+        @pl.when(inner)
+        def _():
+            scatter_z(p, stream, 2, far, z, far).start()
+
+    def scatter_pass(p, stream):
+        @pl.when(inner)
+        def _():
+            scatter_z(p, stream, 0, near, z, near).wait_recv()
+            add_to(partial(p, mate, own_quarter(p, stream)), from_rest(p, z_spot(p, stream, z)))
+            scatter_z(p, stream, 1, mate, z, mate).start()
+
+    def scatter_end(p, stream):
+        scatter_z(p, stream, 0, near, near, near).wait_recv()
+        scatter_z(p, stream, 0, near, mate, near).wait_recv()
+        scatter_z(p, stream, 0, near, z, near).wait_send()
+        scatter_z(p, stream, 1, mate, z, mate).wait_send()
+        block_sum[:, columns(p)] = (
+            partial(p, z, own_quarter(p, stream))[...].astype(F32)
+            + from_rest(p, z_spot(p, stream, near))[...].astype(F32)
+            + from_rest(p, z_spot(p, stream, mate))[...].astype(F32)
+        )
+
+        @pl.when(outer)
+        def _():
+            scatter_z(p, stream, 0, near, far, near).wait_recv()
+            block_sum[:, columns(p)] += from_rest(p, z_spot(p, stream, far))[...].astype(F32)
+
+        scatter_z(p, stream, 2, far, z, far).wait_send()
+
+    def scatter_target(p):
+        piece, start, count = SCATTER_PIECES[p]
+        if piece < 4:
+            return down_sum.at[:, piece * COLS + start : piece * COLS + start + count]
+        if piece < 8:
+            return up_sum.at[:, (piece - 4) * COLS + start : (piece - 4) * COLS + start + count]
+        if piece == 8:
+            return out_sum.at[:, start : start + count]
+        return in_sum.at[piece - 9, :, start : start + count]
+
+    def scatter_stage(p, stage):
+        late = SCATTER_KINDS[p]
+        at_a = scatter_way(p)[0]
+        if stage == 0:
+            scatter_side(p, 0).start()
+            scatter_side(p, 1).start()
+        elif stage == 1:
+            scatter_side(p, 0).wait()
+            scatter_side(p, 1).wait()
+
+            def body(k):
+                add_to(partial(p, k, mine), from_b(p, 0, k))
+                add_to(partial(p, k, at_a), from_b(p, 1, k))
+
+            loop(chain, body)
+            if late:
+                scatter_start(p, 0)
+                scatter_start(p, 1)
+            else:
+                scatter_side(p, 2).start()
+        elif stage == 2:
+            if late:
+                scatter_pass(p, 0)
+                scatter_pass(p, 1)
+            else:
+                scatter_side(p, 2).wait()
+                loop(chain, lambda k: add_to(partial(p, k, mine), from_rest(p, k)))
+                scatter_start(p, 0)
+        elif stage == 3:
+            if late:
+                scatter_end(p, 1)
+                partial(p, z, at_a)[...] = block_sum[:, columns(p)].astype(BF)
+                scatter_side(p, 2).start()
+            else:
+                scatter_pass(p, 0)
         else:
-            scatter_done(p, in_sum, slice((p - 9) * COLS, (p - 8) * COLS))
-
-    def scatter_tick(k):
-        if k < PIECES:
-            scatter_plane(k)
-        if 0 <= k - 1 < PIECES:
-            scatter_z(k - 1)
-        if 0 <= k - 2 < PIECES:
-            finish(k - 2)
+            scatter_end(p, 0)
+            total = block_sum[:, columns(p)]
+            if late:
+                scatter_side(p, 2).wait()
+                total = total + from_rest(p, 2 * chain)[...].astype(F32)
+            scatter_target(p)[...] = total
 
     def gradient(left, right, piece, c):
         def body(m):
@@ -561,15 +890,6 @@
             store[8 + piece, part(m, half), :, :, part(c, TILE)] = block.astype(BF).reshape(half, 4, rows, TILE)
 
         loop(2, body)
-
-    def down_piece(p):
-        loop(2, lambda c: gradient(up_t, hidden[2 * p + c], p, c))
-        scatter_corner(p)
-
-    loop(4, down_piece)
-    gather_done(10)
-    for kind in range(chain - 1):
-        plane_first(kind).wait()
 
     def back_hidden(c):
         at = part(c % 2, TILE)
@@ -585,44 +905,24 @@
         total = lax.fori_loop(0, slots // 64, rows_of, jnp.zeros((8, TILE), F32))
         up_sums[c] = jnp.sum(total, axis=0, keepdims=True)
 
-    loop(8, back_hidden)
-    scatter_tick(0)
-
-    def up_piece(p):
-        loop(2, lambda c: gradient(second_t, slope[2 * p + c], 4 + p, c))
-        scatter_corner(4 + p)
-
-    loop(2, up_piece)
-    scatter_tick(1)
-    loop(4, up_piece, 2)
-    scatter_tick(2)
-
     def mixed(j):
         total = nt(hidden[0], weight_rows(16, j, 0))
         for c in range(1, 8):
             total = total + nt(hidden[c], weight_rows(16 + c // 2, j, c % 2))
         return total
 
-    pair_sum(1, mixed)
-
     def output_rows(i):
         at = part(i, norm_rows)
         values = residual[at, :] + summed(1, at) + output_bias[1:2, :]
-        plain[at, :] = (values * keep_col[at, :]).astype(BF)
-
-    loop(slots // norm_rows, output_rows)
+        plain[at, :] = (values * keep_col[at, 0:1]).astype(BF)
+
     block_local, block_across, block_on = row_back(plain, block_out, 2)
-    block_local.start()
-    block_across.start()
-    scatter_tick(3)
 
     def second_back(j):
         total = nt(slope[0], weight_rows(4, j, 0))
         for c in range(1, 8):
             total = total + nt(slope[c], weight_rows(4 + c // 2, j, c % 2))
         return total
-
-    pair_sum(0, second_back)
 
     def norm_second_back(i):
         at = part(i, norm_rows)
@@ -645,14 +945,11 @@
         sums[2] += fold(total)
         sums[3] += fold(upstream)
 
-    loop(slots // norm_rows, norm_second_back)
-    for j in range(4):
-        for k in range(2):
-            at = j * TILE + k * 128
-            up_t[at : at + 128, :] = hidden[4 + j, :, k * 128 : (k + 1) * 128].T
-    scatter_tick(4)
-    loop(2, lambda c: gradient(up_t, context[c], 8, c))
-    scatter_corner(8)
+    def turn_attend():
+        for j in range(4):
+            for k in range(2):
+                at = j * TILE + k * 128
+                up_t[at : at + 128, :] = hidden[4 + j, :, k * 128 : (k + 1) * 128].T
 
     def back_context(c):
         total = None
@@ -661,10 +958,6 @@
             term = nn(hidden[4 + j], tile)
             total = term if total is None else total + term
         context_grad[c] = total.astype(BF)
-
-    loop(2, back_context)
-    block_across.wait()
-    block_on.start()
 
     def attend_back(pair):
         where_pair = part(pair % 2, 128)
@@ -688,13 +981,14 @@
             total = lax.fori_loop(0, n_chunks, power, jnp.zeros((8, slots), F32))
             centre = jnp.sum(total, axis=0, keepdims=True)
 
+            value_grad = nn(prob_low[...], own_in)
+
             def rest(i):
                 at = part(i, chunk)
-                score_low[at, :] = (score[at, :] * (other[at, :] - centre)).astype(BF)
+                prob_low[at, :] = (score[at, :] * (other[at, :] - centre)).astype(BF)
 
             loop(n_chunks, rest)
-            value_grad = nn(prob_low[...], own_in)
-            key_grad = nn(score_low[...], query)
+            key_grad = nn(prob_low[...], query)
             if h == 0:
                 gather_acc[0] = value_grad
                 gather_acc[1] = key_grad
@@ -702,7 +996,7 @@
                 gather_acc[0] += value_grad
                 gather_acc[1] = jnp.where(own, key_grad, gather_acc[1])
             flip[h * HEAD_DIM : (h + 1) * HEAD_DIM, :] = nn(
-                turned[h * HEAD_DIM : (h + 1) * HEAD_DIM, :], score_low[...]
+                turned[h * HEAD_DIM : (h + 1) * HEAD_DIM, :], prob_low[...]
             ) * (HEAD_DIM**-0.5)
         query_low = flip[...].T.astype(BF)
         value_low = gather_acc[0].astype(BF)
@@ -712,16 +1006,6 @@
         head_sums[0, pair] = jnp.sum(query_low.astype(F32), axis=0, keepdims=True)
         head_sums[1, pair] = jnp.sum(value_low.astype(F32), axis=0, keepdims=True)
 
-    for pair in range(4):
-        attend_back(pair)
-        scatter_tick(5 + pair)
-
-    def in_piece(i):
-        loop(2, lambda c: gradient(first_t, heads[i, c], 9 + i, c))
-        scatter_corner(9 + i)
-
-    loop(3, in_piece)
-
     def first_back(j):
         total = None
         for i in range(3):
@@ -729,9 +1013,6 @@
                 term = nt(heads[i, c], weight_rows(i, j, c))
                 total = term if total is None else total + term
         return total
-
-    pair_sum(1, first_back)
-    scatter_tick(9)
 
     def norm_first_back(i):
         at = part(i, norm_rows)
@@ -747,25 +1028,24 @@
         sums[4] += fold(incoming * scaled)
         sums[5] += fold(incoming)
 
-    loop(slots // norm_rows, norm_first_back)
     grad_local, grad_across, grad_on = row_back(row_in, token_grad, 3)
-    grad_local.start()
-    grad_across.start()
 
     def collapse(k):
         return jnp.sum(sums[k], axis=0, keepdims=True)
 
-    small[0:1, :] = collapse(4)
-    small[1:2, :] = collapse(5)
-    small[2:3, :] = jnp.concatenate([head_sums[i, k] for i in range(2) for k in range(4)], axis=1)
-    small[3:4, :] = collapse(2)
-    small[4:5, :] = collapse(3)
-    small[5:6, :] = collapse(0)
-    small[6:7, :] = collapse(1)
-    small[7:8, :] = jnp.concatenate([up_sums[k] for k in range(4)], axis=1)
-    small[8:9, :] = jnp.concatenate([up_sums[4 + k] for k in range(4)], axis=1)
-    small[9:10, :] = jnp.concatenate([peak_out[0:1, :]] * 8, axis=1)
-    small[10:16, :] = jnp.zeros((6, small.shape[1]), F32)
+    def small_fill():
+        small[0:1, :] = collapse(4)
+        small[1:2, :] = collapse(5)
+        small[2:3, :] = jnp.concatenate([head_sums[i, k] for i in range(2) for k in range(4)], axis=1)
+        small[3:4, :] = collapse(2)
+        small[4:5, :] = collapse(3)
+        small[5:6, :] = collapse(0)
+        small[6:7, :] = collapse(1)
+        small[7:8, :] = jnp.concatenate([up_sums[k] for k in range(4)], axis=1)
+        small[8:9, :] = jnp.concatenate([up_sums[4 + k] for k in range(4)], axis=1)
+        small[9:10, :] = jnp.concatenate([peaks[0:1, :]] * 8, axis=1)
+        small[10:16, :] = jnp.zeros((6, small.shape[1]), F32)
+
     row_index = lax.broadcasted_iota(jnp.int32, small.shape, 0)
 
     def joined(left, right):
@@ -775,32 +1055,148 @@
         return remote(source, target, small_send.at[k], small_recv.at[k], device)
 
     over_x = small_copy(small, small_x.at[0], 0, to_x)
-    over_x.start()
-    scatter_tick(10)
-    over_x.wait()
-    small_x[1] = joined(small[...], small_x[0])
     over_y = small_copy(small_x.at[1], small_y, 1, to_y)
-    over_y.start()
-    grad_across.wait()
-    grad_on.start()
-    scatter_tick(11)
-    over_y.wait()
-    small_z[z] = joined(small_x[1], small_y[...])
-    over_z = [small_copy(small_z.at[z], small_z.at[z], 1 + step, to_z(step)) for step in range(1, chain)]
-    for copy in over_z:
-        copy.start()
-    scatter_tick(12)
-    for copy in over_z:
-        copy.wait()
-    total = small_z[0]
-    for k in range(1, chain):
-        total = joined(total, small_z[k])
-    small_out[...] = total
-    scatter_tick(13)
-    block_local.wait()
-    block_on.wait()
-    grad_local.wait()
-    grad_on.wait()
+    along_z = [
+        small_copy(small_z.at[z], small_z.at[z], 1 + step, to_z((z + step) % chain)) for step in range(1, chain)
+    ]
+
+    def small_stage(stage):
+        if stage == 0:
+            small_fill()
+            over_x.start()
+        elif stage == 1:
+            over_x.wait()
+            small_x[1] = joined(small[...], small_x[0])
+            over_y.start()
+        elif stage == 2:
+            over_y.wait()
+            small_z[z] = joined(small_x[1], small_y[...])
+            for copy in along_z:
+                copy.start()
+        else:
+            for copy in along_z:
+                copy.wait()
+            total = small_z[0]
+            for k in range(1, chain):
+                total = joined(total, small_z[k])
+            small_out[...] = total
+
+    rows_over = {
+        TOKENS: (token_local, token_across, token_on),
+        COTANGENT: (up_local, up_across, up_on),
+        BLOCK: (block_local, block_across, block_on),
+        GRADIENT: (grad_local, grad_across, grad_on),
+    }
+
+    def rows_stage(which, stage):
+        local, across, onward = rows_over[which]
+        if stage == 0:
+            local.start()
+            across.start()
+        elif stage == 1:
+            across.wait()
+            onward.start()
+        else:
+            onward.wait()
+            local.wait()
+
+    def norms(slot, body):
+        pair_wait(slot)
+        loop(slots // norm_rows, body)
+
+    def mask_and_turn():
+        loop(slots // 64, mask_rows)
+        turn(row_up, up_t)
+
+    compute = {
+        NORM_ONE: lambda i: (prepare(), loop(slots // norm_rows, norm_first)),
+        TURN_ONE: lambda i: turn(plain, first_t),
+        PROJECT: lambda i: loop(2, lambda c: project(c, i)),
+        ATTEND: attend,
+        SEND_ONE: lambda i: pair_sum(0, attended),
+        NORM_TWO: lambda i: norms(0, norm_second),
+        TURN_TWO: lambda i: turn(plain, second_t),
+        ACTIVATE: lambda i: loop(2 * i + 2, activate, 2 * i),
+        MASK: lambda i: mask_and_turn(),
+        GRAD_DOWN: lambda i: loop(2, lambda c: gradient(up_t, hidden[2 * i + c], i, c)),
+        BACK_HIDDEN: lambda i: loop(2 * i + 2, back_hidden, 2 * i),
+        GRAD_UP: lambda i: loop(2, lambda c: gradient(second_t, slope[2 * i + c], 4 + i, c)),
+        SEND_TWO: lambda i: pair_sum(1, mixed),
+        OUTPUT: lambda i: norms(1, output_rows),
+        SEND_THREE: lambda i: pair_sum(0, second_back),
+        BACK_TWO: lambda i: norms(0, norm_second_back),
+        TURN_BACK: lambda i: turn_attend(),
+        GRAD_OUT: lambda i: loop(2, lambda c: gradient(up_t, context[c], 8, c)),
+        BACK_CONTEXT: lambda i: loop(2, back_context),
+        ATTEND_BACK: attend_back,
+        GRAD_IN: lambda i: gradient(first_t, heads[i // 2, i % 2], 9 + i // 2, i % 2),
+        SEND_FOUR: lambda i: pair_sum(1, first_back),
+        BACK_ONE: lambda i: norms(1, norm_first_back),
+    }
+    for kind, which, index in SCHEDULE:
+        if kind == GATHER:
+            gather_stage(which, index)
+        elif kind == SCATTER:
+            scatter_stage(which, index)
+        elif kind == ROWS:
+            rows_stage(which, index)
+        elif kind == SMALL:
+            small_stage(index)
+        else:
+            compute[which](index)
+
+
+def finish_kernel(
+    block_in,
+    grad_in,
+    in_sum,
+    out_sum,
+    up_sum,
+    down_sum,
+    small,
+    weight,
+    block_out,
+    grad_out,
+    first_gain,
+    first_shift,
+    in_out,
+    in_bias,
+    out_out,
+    out_bias,
+    second_gain,
+    second_shift,
+    up_out,
+    up_bias,
+    down_out,
+    clipped,
+    factor,
+):
+    block_out[...] = block_in[...]
+    grad_out[...] = grad_in[...].astype(F32)
+    out_out[...] = out_sum[...]
+    up_out[...] = up_sum[...]
+    down_out[...] = down_sum[...]
+    local = out_sum.shape[1]
+    in_out[...] = in_sum[...]
+    first_gain[...] = small[0, :]
+    first_shift[...] = small[1, :]
+    in_bias[0:1, :] = small[2:3, 0:local]
+    in_bias[1:2, :] = small[2:3, local:]
+    out_bias[...] = small[3:5, :]
+    second_gain[...] = small[5, :]
+    second_shift[...] = small[6, :]
+    width = small.shape[1]
+    up_bias[0:width] = small[7, :]
+    up_bias[width:] = small[8, :]
+    factors = CLIP_LIMIT / jnp.maximum(small[9:10, 0:128], CLIP_LIMIT)
+    factor[...] = factors[0, 0 : factor.shape[0]]
+    roots = jnp.sqrt(factors)
+    head = lax.broadcasted_iota(jnp.int32, (1, local), 1) // HEAD_DIM
+    scale = jnp.zeros((1, local), F32)
+    for h in range(local // HEAD_DIM):
+        scale = jnp.where(head == h, roots[:, h : h + 1], scale)
+    for k in range(2):
+        clipped[:, k, :] = weight[k].astype(F32) * scale
 
 
 def on_device_fused(
@@ -823,28 +1219,25 @@
     group, tok_rows, width = tokens.shape
     slots = segments.shape[1]
     rows = input_weight.shape[0]
-    flags = lax.dynamic_slice_in_dim(segments, lax.axis_index("context"), 1, 0).astype(F32)
-    bias_three = jnp.stack([input_bias[0], jnp.zeros_like(input_bias[0]), input_bias[1]])[:, None, :]
+    weights = jnp.transpose(input_weight, (1, 0, 2))
     operands = (
         tokens,
         cotangent,
-        input_weight.reshape(rows, -1),
+        segments,
+        weights,
         output_weight,
         up_weight,
         down_weight,
         first_gain[None],
         first_shift[None],
-        bias_three,
+        input_bias,
         output_bias,
         second_gain[None],
         second_shift[None],
-        up_bias.reshape(8, 1, TILE),
-        flags.reshape(slots, 1),
-        flags,
+        up_bias[None],
     )
     anywhere = pl.BlockSpec(memory_space=pl.ANY)
     vmem = pl.BlockSpec(memory_space=pltpu.VMEM)
-    half = chain // 2
     block = (rows, COLS)
     dma = pltpu.SemaphoreType.DMA
     results = pl.pallas_call(
@@ -852,20 +1245,18 @@
         out_shape=(
             jax.ShapeDtypeStruct(tokens.shape, BF),
             jax.ShapeDtypeStruct(tokens.shape, BF),
-            jax.ShapeDtypeStruct((rows, 3 * COLS), F32),
+            jax.ShapeDtypeStruct((3, rows, COLS), F32),
             jax.ShapeDtypeStruct((rows, COLS), F32),
             jax.ShapeDtypeStruct((rows, 4 * COLS), F32),
             jax.ShapeDtypeStruct((rows, 4 * COLS), F32),
             jax.ShapeDtypeStruct((16, width), F32),
-            jax.ShapeDtypeStruct((8, 128), F32),
         ),
-        in_specs=[anywhere] * 6 + [vmem] * 9,
-        out_specs=[anywhere] * 2 + [vmem] * 6,
+        in_specs=[anywhere] * 2 + [vmem] + [anywhere] * 4 + [vmem] * 7,
+        out_specs=[anywhere] * 2 + [vmem] * 5,
         scratch_shapes=[
             pltpu.VMEM((20, chain, 4) + block, BF),
-            pltpu.VMEM((PIECES, 2, half) + block, BF),
             pltpu.VMEM((PIECES, 2, chain) + block, BF),
-            pltpu.VMEM((PIECES, chain - 1) + block, BF),
+            pltpu.VMEM((PIECES, 2 * chain + 1) + block, BF),
             pltpu.VMEM((slots, width), BF),
             pltpu.VMEM((slots, width), BF),
             pltpu.VMEM((slots, width), BF),
@@ -883,7 +1274,6 @@
             pltpu.VMEM((slots, slots), F32),
             pltpu.VMEM((slots, slots), F32),
             pltpu.VMEM((slots, slots), BF),
-            pltpu.VMEM((slots, slots), BF),
             pltpu.VMEM((128, slots), F32),
             pltpu.VMEM((128, slots), BF),
             pltpu.VMEM((2, slots, 128), F32),
@@ -895,11 +1285,15 @@
             pltpu.VMEM((2, 16, width), F32),
             pltpu.VMEM((16, width), F32),
             pltpu.VMEM((chain, 16, width), F32),
-            dma((PIECES, 7)),
-            dma((PIECES, 7)),
+            pltpu.VMEM((slots, 128), F32),
+            pltpu.VMEM((1, slots), F32),
+            pltpu.VMEM((8, 128), F32),
+            pltpu.VMEM(block, F32),
+            dma((len(GATHER_PIECES), 11)),
+            dma((len(GATHER_PIECES), 11)),
             dma((PIECES,)),
-            dma((PIECES, 7)),
-            dma((PIECES, 7)),
+            dma((len(SCATTER_PIECES), 11)),
+            dma((len(SCATTER_PIECES), 11)),
             dma((4,)),
             dma((2, 4)),
             dma((4, 3)),
@@ -912,29 +1306,32 @@
         ),
         name="layer",
     )(*operands)
-    block_output, tokens_gradient, in_sum, out_sum, up_sum, down_sum, small, _ = results
-    count = input_weight.shape[2] // HEAD_DIM
-    factor = CLIP_LIMIT / jnp.maximum(small[9, :count], CLIP_LIMIT)
-    column_scale = jnp.repeat(jnp.sqrt(factor), HEAD_DIM)
-    clipped_weight = input_weight[:, :2, :].astype(F32) * column_scale[None, None, :]
-    local_width = input_weight.shape[2]
-    return (
-        block_output,
-        tokens_gradient.astype(F32),
-        small[0],
-        small[1],
-        in_sum.reshape(rows, 3, local_width),
-        small[2].reshape(2, local_width),
-        out_sum,
-        small[3:5],
-        small[5],
-        small[6],
-        up_sum,
-        small[7:9].reshape(-1),
-        down_sum,
-        clipped_weight,
-        factor,
-    )
+    local = input_weight.shape[2]
+    flat = jax.ShapeDtypeStruct((width,), F32)
+    finished = pl.pallas_call(
+        finish_kernel,
+        out_shape=(
+            jax.ShapeDtypeStruct(tokens.shape, BF),
+            jax.ShapeDtypeStruct(tokens.shape, F32),
+            flat,
+            flat,
+            jax.ShapeDtypeStruct(weights.shape, F32),
+            jax.ShapeDtypeStruct(input_bias.shape, F32),
+            jax.ShapeDtypeStruct((rows, local), F32),
+            jax.ShapeDtypeStruct(output_bias.shape, F32),
+            flat,
+            flat,
+            jax.ShapeDtypeStruct(up_weight.shape, F32),
+            jax.ShapeDtypeStruct(up_bias.shape, F32),
+            jax.ShapeDtypeStruct(down_weight.shape, F32),
+            jax.ShapeDtypeStruct((rows, 2, local), F32),
+            jax.ShapeDtypeStruct((local // HEAD_DIM,), F32),
+        ),
+        in_specs=[vmem] * 8,
+        out_specs=[vmem] * 15,
+        name="finish",
+    )(*results, weights)
+    return finished[:4] + (jnp.transpose(finished[4], (1, 0, 2)),) + finished[5:]
 
 
 def on_device(

time: 280 us -> 230 us (0.82)
  Pallas kernels: 261 us -> 227 us
  local copies, waits for them, and re-layouts: 10.8 us -> 0 us
  other arithmetic: 6.56 us -> 0 us
    pallas_call x1, Pallas kernels: 261 us -> 222 us  [on_device_fused(): pl.pallas_call(functools.partial(layer_kernel, chain), out_shape=(jax.Sha...]
    pallas_call x0 -> x1, Pallas kernels: none -> 4.89 us  [on_device_fused(): pl.pallas_call(finish_kernel, out_shape=(jax.ShapeDtypeStruct(tokens.shap...]
    unnamed x21 -> x0, local copies, waits for them, and re-layouts: 4.7 us -> none
    convert_element_type x2 -> x0, other arithmetic: 4.46 us -> none  [the longest x1 3.19 us: on_device_fused(): tokens_gradient.astype(F32)]
    reshape x3 -> x0, local copies, waits for them, and re-layouts: 3.3 us -> none  [the longest x1 1.62 us: on_device_fused(): input_weight.reshape(rows, -1)]
where the time goes in v2:
time: 230 us; the launch traced here: 228 us
  Pallas kernels  227 us (99%)
    pallas_call x1, Pallas kernels, on_device_fused(): pl.pallas_call(functools.partial(layer_kernel, chain), out_shape=(jax.Sha...  222 us
    pallas_call x1, Pallas kernels, on_device_fused(): pl.pallas_call(finish_kernel, out_shape=(jax.ShapeDtypeStruct(tokens.shap...  4.89 us

profile of v2, /device:TPU:0, one launch (start us, length us, event | category | flops | bytes accessed | tf_op | source)
XLA Modules:
  0.0 227.8 jit_solution(3770555159061641888)
XLA Ops:
  0.7 222.0 %layer.1 = (bf16[2,320,1024]{2,1,0:T(8,128)(2,1)}, bf16[2,320,1024]{2,1,0:T(8,128)(2,1)}, f32[3,64,512]{2,1,0:T(8,128)}, f32[64,512]{1,0:T(8,128)}, f32[64,2048]...) custom-call(bf16[2,320,1024]{2,1,0:T(8,128)(2,1)} %tokens.1, bf16[2,320,1024]{2,1,0:T(8,128)(2,1)} %cotangent.1, ...), custom_call_target="tpu_custom_call" | custom-call | tf_op jit(solution)/shard_map/layer/pallas_call | solution.py:1243
  222.7 4.9 %finish.1 = (bf16[2,320,1024]{2,1,0:T(8,128)(2,1)}, f32[2,320,1024]{2,1,0:T(8,128)}, f32[1024]{0:T(1024)}, f32[1024]{0:T(1024)}, f32[3,64,512]{2,1,0:T(8,128)}, ...) custom-call(bf16[2,320,1024]{2,1,0:T(8,128)(2,1)} %get-tuple-element, ...), custom_call_target="tpu_custom_call" | custom-call | tf_op jit(solution)/shard_map/finish/pallas_call | solution.py:1311

commit v3 on v2

--- a/solution.py
+++ b/solution.py
@@ -90,10 +90,10 @@
     (11, 0, 256),
     (11, 256, 256),
 )
-GATHER_KINDS = (0, 1, 0, 0, 1, 1, 0, 0, 1, 0, 0, 1, 1)
-SCATTER_KINDS = (1, 1, 1, 0, 1, 1, 0, 1, 1, 0, 0, 0, 0, 0)
-GATHER_SWAPPED = (0, 0, 0, 1, 0, 0, 0, 0, 0, 0, 0, 0, 0)
-SCATTER_SWAPPED = (0, 0, 0, 0, 0, 0, 1, 0, 0, 0, 1, 0, 0, 0)
+GATHER_KINDS = (0, 0, 0, 0, 0, 1, 0, 1, 1, 1, 0, 0, 2)
+SCATTER_KINDS = (1, 1, 1, 1, 2, 1, 0, 0, 1, 0, 0, 1, 0, 0)
+GATHER_SWAPPED = (0, 1, 0, 1, 0, 0, 0, 0, 0, 0, 0, 0, 0)
+SCATTER_SWAPPED = (0, 0, 0, 0, 0, 0, 0, 0, 0, 0, 1, 1, 0, 0)
 GATHER, SCATTER, ROWS, SMALL, COMPUTE = range(5)
 TOKENS, COTANGENT, BLOCK, GRADIENT = range(4)
 (
@@ -122,94 +122,86 @@
     BACK_ONE,
 ) = range(23)
 SCHEDULE = (
-    (GATHER, 0, 0),
     (GATHER, 3, 0),
     (ROWS, TOKENS, 0),
-    (GATHER, 7, 0),
+    (GATHER, 2, 0),
+    (GATHER, 0, 0),
+    (GATHER, 3, 1),
+    (GATHER, 3, 2),
+    (GATHER, 2, 1),
+    (GATHER, 2, 2),
+    (GATHER, 4, 0),
+    (GATHER, 1, 0),
     (GATHER, 0, 1),
     (GATHER, 0, 2),
-    (GATHER, 3, 1),
-    (GATHER, 3, 2),
-    (GATHER, 2, 0),
-    (GATHER, 7, 1),
+    (GATHER, 5, 0),
+    (GATHER, 3, 3),
     (GATHER, 6, 0),
-    (GATHER, 1, 0),
-    (GATHER, 8, 0),
-    (GATHER, 7, 2),
+    (GATHER, 2, 3),
+    (GATHER, 4, 1),
+    (GATHER, 4, 2),
+    (GATHER, 0, 3),
+    (GATHER, 9, 0),
+    (GATHER, 10, 0),
     (ROWS, TOKENS, 1),
+    (GATHER, 1, 1),
+    (GATHER, 1, 2),
+    (GATHER, 1, 3),
+    (GATHER, 2, 4),
+    (GATHER, 6, 1),
+    (GATHER, 9, 1),
+    (GATHER, 12, 0),
+    (GATHER, 5, 1),
+    (GATHER, 3, 4),
+    (ROWS, COTANGENT, 0),
     (ROWS, TOKENS, 2),
     (COMPUTE, NORM_ONE, 0),
-    (GATHER, 3, 3),
-    (ROWS, COTANGENT, 0),
-    (GATHER, 1, 1),
-    (GATHER, 7, 3),
-    (GATHER, 2, 1),
-    (GATHER, 2, 2),
+    (COMPUTE, PROJECT, 2),
+    (COMPUTE, PROJECT, 1),
+    (GATHER, 11, 0),
+    (GATHER, 4, 3),
+    (GATHER, 6, 2),
     (COMPUTE, TURN_ONE, 0),
-    (GATHER, 0, 3),
-    (GATHER, 8, 1),
-    (GATHER, 9, 0),
-    (GATHER, 1, 2),
-    (GATHER, 1, 3),
-    (GATHER, 2, 3),
-    (GATHER, 8, 2),
-    (GATHER, 8, 3),
-    (GATHER, 4, 0),
-    (GATHER, 4, 1),
-    (GATHER, 3, 4),
+    (GATHER, 7, 0),
     (GATHER, 0, 4),
-    (GATHER, 7, 4),
-    (GATHER, 9, 1),
-    (GATHER, 9, 2),
-    (GATHER, 10, 0),
-    (COMPUTE, PROJECT, 2),
-    (ROWS, COTANGENT, 1),
-    (ROWS, COTANGENT, 2),
-    (COMPUTE, MASK, 0),
-    (GATHER, 2, 4),
-    (COMPUTE, PROJECT, 1),
-    (GATHER, 5, 0),
-    (GATHER, 4, 2),
-    (GATHER, 4, 3),
-    (GATHER, 10, 1),
-    (GATHER, 10, 2),
-    (GATHER, 9, 3),
-    (GATHER, 6, 1),
-    (GATHER, 6, 2),
-    (GATHER, 11, 0),
-    (GATHER, 5, 1),
-    (GATHER, 12, 0),
     (GATHER, 1, 4),
     (COMPUTE, PROJECT, 0),
     (COMPUTE, ATTEND, 0),
-    (COMPUTE, ATTEND, 1),
-    (COMPUTE, ATTEND, 2),
-    (COMPUTE, ATTEND, 3),
     (GATHER, 5, 2),
     (GATHER, 5, 3),
+    (ROWS, COTANGENT, 1),
+    (GATHER, 4, 4),
+    (GATHER, 12, 1),
+    (GATHER, 8, 0),
+    (COMPUTE, ATTEND, 1),
     (GATHER, 11, 1),
-    (GATHER, 6, 3),
-    (GATHER, 12, 1),
-    (GATHER, 4, 4),
+    (GATHER, 11, 2),
+    (GATHER, 9, 2),
+    (GATHER, 9, 3),
+    (COMPUTE, ATTEND, 3),
+    (ROWS, COTANGENT, 2),
+    (COMPUTE, MASK, 0),
+    (GATHER, 10, 1),
+    (GATHER, 10, 2),
+    (GATHER, 7, 1),
+    (GATHER, 8, 1),
+    (COMPUTE, ATTEND, 2),
     (COMPUTE, SEND_ONE, 0),
     (COMPUTE, NORM_TWO, 0),
-    (COMPUTE, ACTIVATE, 2),
-    (COMPUTE, GRAD_DOWN, 2),
-    (SCATTER, 2, 0),
     (COMPUTE, TURN_TWO, 0),
+    (GATHER, 8, 2),
+    (GATHER, 6, 3),
+    (GATHER, 10, 3),
+    (GATHER, 7, 2),
+    (GATHER, 7, 3),
+    (GATHER, 12, 2),
+    (GATHER, 12, 3),
+    (GATHER, 11, 3),
+    (GATHER, 8, 3),
     (GATHER, 5, 4),
     (COMPUTE, ACTIVATE, 0),
     (COMPUTE, GRAD_DOWN, 0),
     (SCATTER, 0, 0),
-    (GATHER, 10, 3),
-    (GATHER, 11, 2),
-    (GATHER, 11, 3),
-    (GATHER, 8, 4),
-    (COMPUTE, ACTIVATE, 3),
-    (COMPUTE, GRAD_DOWN, 3),
-    (GATHER, 12, 2),
-    (GATHER, 12, 3),
-    (SCATTER, 2, 1),
     (GATHER, 9, 4),
     (COMPUTE, BACK_HIDDEN, 0),
     (COMPUTE, GRAD_UP, 0),
@@ -218,109 +210,117 @@
     (COMPUTE, ACTIVATE, 1),
     (COMPUTE, GRAD_DOWN, 1),
     (SCATTER, 1, 0),
+    (GATHER, 7, 4),
+    (COMPUTE, ACTIVATE, 2),
+    (COMPUTE, GRAD_DOWN, 2),
+    (SCATTER, 2, 0),
     (GATHER, 10, 4),
     (COMPUTE, BACK_HIDDEN, 1),
     (COMPUTE, GRAD_UP, 1),
     (SCATTER, 5, 0),
     (GATHER, 11, 4),
-    (COMPUTE, BACK_HIDDEN, 2),
-    (COMPUTE, GRAD_UP, 2),
-    (SCATTER, 6, 0),
-    (SCATTER, 0, 1),
+    (GATHER, 8, 4),
+    (COMPUTE, ACTIVATE, 3),
+    (COMPUTE, GRAD_DOWN, 3),
     (GATHER, 12, 4),
     (COMPUTE, SEND_TWO, 0),
     (COMPUTE, BACK_HIDDEN, 3),
     (COMPUTE, GRAD_UP, 3),
     (SCATTER, 7, 0),
-    (COMPUTE, OUTPUT, 0),
-    (COMPUTE, SEND_THREE, 0),
-    (ROWS, BLOCK, 0),
     (SCATTER, 3, 0),
     (SCATTER, 1, 1),
-    (SCATTER, 2, 2),
+    (COMPUTE, OUTPUT, 0),
+    (COMPUTE, BACK_HIDDEN, 2),
+    (COMPUTE, SEND_THREE, 0),
+    (COMPUTE, GRAD_UP, 2),
+    (SCATTER, 6, 0),
+    (SCATTER, 0, 1),
+    (SCATTER, 5, 1),
     (SCATTER, 4, 1),
-    (SCATTER, 0, 2),
+    (SCATTER, 1, 2),
+    (SCATTER, 2, 1),
     (COMPUTE, BACK_TWO, 0),
     (COMPUTE, BACK_CONTEXT, 0),
+    (COMPUTE, ATTEND_BACK, 1),
     (COMPUTE, ATTEND_BACK, 2),
-    (COMPUTE, ATTEND_BACK, 1),
     (COMPUTE, TURN_BACK, 0),
     (SCATTER, 7, 1),
-    (SCATTER, 6, 1),
     (COMPUTE, GRAD_OUT, 0),
     (SCATTER, 8, 0),
-    (SCATTER, 1, 2),
+    (SCATTER, 5, 2),
+    (SCATTER, 0, 2),
+    (COMPUTE, ATTEND_BACK, 0),
+    (ROWS, BLOCK, 0),
     (SCATTER, 3, 1),
-    (SCATTER, 5, 1),
-    (SCATTER, 4, 2),
+    (SCATTER, 7, 2),
     (COMPUTE, ATTEND_BACK, 3),
-    (COMPUTE, ATTEND_BACK, 0),
     (COMPUTE, GRAD_IN, 3),
     (SCATTER, 11, 0),
-    (COMPUTE, SEND_FOUR, 0),
-    (COMPUTE, GRAD_IN, 1),
     (COMPUTE, GRAD_IN, 5),
     (SCATTER, 13, 0),
-    (SCATTER, 7, 2),
-    (SCATTER, 8, 1),
-    (SCATTER, 3, 2),
+    (COMPUTE, SEND_FOUR, 0),
+    (COMPUTE, GRAD_IN, 0),
     (COMPUTE, GRAD_IN, 4),
     (SCATTER, 12, 0),
-    (SCATTER, 6, 2),
+    (COMPUTE, GRAD_IN, 1),
+    (SCATTER, 9, 0),
+    (SCATTER, 3, 2),
     (SCATTER, 11, 1),
-    (COMPUTE, GRAD_IN, 0),
-    (SCATTER, 9, 0),
-    (SCATTER, 5, 2),
+    (SCATTER, 4, 2),
+    (SCATTER, 6, 1),
+    (SCATTER, 2, 2),
+    (SCATTER, 8, 1),
     (COMPUTE, BACK_ONE, 0),
-    (ROWS, GRADIENT, 0),
     (SMALL, 0, 0),
     (SMALL, 0, 1),
-    (SCATTER, 8, 2),
-    (SCATTER, 12, 1),
-    (SCATTER, 9, 1),
+    (ROWS, GRADIENT, 0),
+    (SCATTER, 6, 2),
+    (SCATTER, 7, 3),
+    (ROWS, BLOCK, 1),
+    (SCATTER, 13, 1),
     (COMPUTE, GRAD_IN, 2),
     (SCATTER, 10, 0),
-    (SCATTER, 3, 3),
-    (SCATTER, 13, 1),
-    (SCATTER, 0, 3),
-    (ROWS, BLOCK, 1),
-    (SCATTER, 5, 3),
-    (SCATTER, 11, 2),
-    (SCATTER, 11, 3),
     (SMALL, 0, 2),
+    (SCATTER, 10, 1),
+    (SCATTER, 9, 1),
+    (SCATTER, 8, 2),
+    (SCATTER, 1, 3),
     (ROWS, GRADIENT, 1),
     (ROWS, GRADIENT, 2),
-    (SCATTER, 7, 3),
+    (SCATTER, 13, 2),
+    (SCATTER, 13, 3),
+    (SCATTER, 5, 3),
+    (SCATTER, 4, 3),
+    (SCATTER, 11, 2),
+    (SCATTER, 10, 2),
+    (SCATTER, 10, 3),
+    (SCATTER, 0, 3),
+    (SCATTER, 12, 1),
+    (SCATTER, 9, 2),
+    (SCATTER, 3, 3),
+    (SCATTER, 6, 3),
+    (SCATTER, 8, 3),
     (SCATTER, 2, 3),
+    (ROWS, BLOCK, 2),
+    (SCATTER, 13, 4),
+    (SCATTER, 0, 4),
+    (SCATTER, 5, 4),
+    (SMALL, 0, 3),
+    (SCATTER, 1, 4),
+    (SCATTER, 9, 3),
+    (SCATTER, 11, 3),
+    (SCATTER, 11, 4),
     (SCATTER, 12, 2),
     (SCATTER, 12, 3),
-    (SCATTER, 9, 2),
-    (SCATTER, 10, 1),
-    (SCATTER, 6, 3),
-    (SCATTER, 8, 3),
-    (SCATTER, 8, 4),
-    (SCATTER, 10, 2),
-    (SCATTER, 1, 3),
-    (SCATTER, 4, 3),
-    (SCATTER, 13, 2),
-    (SCATTER, 0, 4),
-    (SCATTER, 10, 3),
+    (SCATTER, 10, 4),
+    (SCATTER, 3, 4),
     (SCATTER, 2, 4),
-    (SMALL, 0, 3),
-    (SCATTER, 3, 4),
-    (SCATTER, 13, 3),
-    (ROWS, BLOCK, 2),
-    (SCATTER, 9, 3),
-    (SCATTER, 1, 4),
     (SCATTER, 4, 4),
     (SCATTER, 7, 4),
+    (SCATTER, 8, 4),
+    (SCATTER, 9, 4),
+    (SCATTER, 6, 4),
     (SCATTER, 12, 4),
-    (SCATTER, 5, 4),
-    (SCATTER, 11, 4),
-    (SCATTER, 10, 4),
-    (SCATTER, 13, 4),
-    (SCATTER, 6, 4),
-    (SCATTER, 9, 4),
 )
 
 
@@ -372,8 +372,8 @@
     down_sum,
     small_out,
     store,
-    over_b,
-    over_rest,
+    over,
+    over_extra,
     row_in,
     row_up,
     plain,
@@ -495,7 +495,10 @@
         return swapped_sides if GATHER_SWAPPED[j] else normal_sides
 
     def gather_z(j, stream, source, slot, target):
-        block = gathered(j, source, gather_way(j)[0] if stream else mine)
+        if GATHER_KINDS[j] == 2:
+            block = gathered(j, source, slice(None))
+        else:
+            block = gathered(j, source, gather_way(j)[0] if stream else mine)
         return remote(
             block,
             block,
@@ -535,13 +538,10 @@
 
     def gather_side(j, kind):
         at_a, _, to_a, to_b = gather_way(j)
-        everything = slice(None)
-        if kind == 0:
-            block, device = gathered(j, z if GATHER_KINDS[j] else everything, mine), to_a
-        elif kind == 1:
-            block, device = gathered(j, everything, mine), to_b
-        else:
-            block, device = gathered(j, everything, at_a), to_b
+        first = kind == 0 and GATHER_KINDS[j] == 1
+        at = z if first or GATHER_KINDS[j] == 2 else slice(None)
+        block = gathered(j, at, at_a if kind == 2 else mine)
+        device = to_b if kind else to_a
         return remote(block, block, gather_send.at[j, 8 + kind], gather_recv.at[j, 8 + kind], device)
 
     def gather_stage(j, stage):
@@ -549,7 +549,22 @@
         if piece not in loaded:
             load(piece).wait()
             loaded.add(piece)
-        if stage == 4:
+        if GATHER_KINDS[j] == 2:
+            if stage == 0:
+                gather_side(j, 0).start()
+                gather_side(j, 1).start()
+            elif stage == 1:
+                gather_side(j, 0).wait()
+                gather_side(j, 2).start()
+            elif stage == 2:
+                gather_side(j, 1).wait()
+                gather_side(j, 2).wait()
+                gather_start(j, 0)
+            elif stage == 3:
+                gather_pass(j, 0)
+            else:
+                gather_end(j, 0)
+        elif stage == 4:
             gather_side(j, 1).wait()
             gather_side(j, 2).wait()
         elif GATHER_KINDS[j]:
@@ -759,30 +774,41 @@
         return store.at[8 + SCATTER_PIECES[p][0], at, quarter_at, :, columns(p)]
 
     def from_b(p, which, at):
-        return over_b.at[SCATTER_PIECES[p][0], which, at, :, columns(p)]
+        if SCATTER_KINDS[p] == 2:
+            return over_extra.at[which, :, columns(p)]
+        if at is None:
+            return over.at[SCATTER_PIECES[p][0], which * chain : (which + 1) * chain, :, columns(p)]
+        return over.at[SCATTER_PIECES[p][0], which * chain + at, :, columns(p)]
 
     def from_rest(p, at):
-        return over_rest.at[SCATTER_PIECES[p][0], at, :, columns(p)]
+        if at is None:
+            return over.at[SCATTER_PIECES[p][0], 2 * chain : 3 * chain, :, columns(p)]
+        return over.at[SCATTER_PIECES[p][0], 2 * chain + at, :, columns(p)]
 
     def scatter_side(p, kind):
         at_a, at_b, to_a, to_b = scatter_way(p)
         sems = (scatter_send.at[p, kind], scatter_recv.at[p, kind])
-        everything = slice(None)
-        if kind == 0:
-            return remote(partial(p, everything, at_b), from_b(p, 0, everything), *sems, to_b)
-        if kind == 1:
-            return remote(partial(p, everything, at_ab), from_b(p, 1, everything), *sems, to_b)
+        at = z if SCATTER_KINDS[p] == 2 else slice(None)
+        if kind < 2:
+            return remote(partial(p, at, at_ab if kind else at_b), from_b(p, kind, None), *sems, to_b)
         if SCATTER_KINDS[p]:
             return remote(partial(p, z, at_a), from_rest(p, 2 * chain), *sems, to_a)
-        return remote(partial(p, everything, at_a), from_rest(p, slice(0, chain)), *sems, to_a)
+        return remote(partial(p, at, at_a), from_rest(p, None), *sems, to_a)
 
     def own_quarter(p, stream):
+        if SCATTER_KINDS[p] == 2:
+            return slice(None)
         return scatter_way(p)[0] if stream else mine
+
+    def from_z(p, stream, spot):
+        if SCATTER_KINDS[p] == 2:
+            return over.at[SCATTER_PIECES[p][0], pl.ds(4 * spot, 4), :, columns(p)]
+        return from_rest(p, z_spot(p, stream, spot))
 
     def scatter_z(p, stream, slot, block, spot, target):
         return remote(
             partial(p, block, own_quarter(p, stream)),
-            from_rest(p, z_spot(p, stream, spot)),
+            from_z(p, stream, spot),
             scatter_send.at[p, 3 + 4 * stream + slot],
             scatter_recv.at[p, 3 + 4 * stream + spot],
             to_z(target),
@@ -810,7 +836,7 @@
         @pl.when(inner)
         def _():
             scatter_z(p, stream, 0, near, z, near).wait_recv()
-            add_to(partial(p, mate, own_quarter(p, stream)), from_rest(p, z_spot(p, stream, z)))
+            add_to(partial(p, mate, own_quarter(p, stream)), from_z(p, stream, z))
             scatter_z(p, stream, 1, mate, z, mate).start()
 
     def scatter_end(p, stream):
@@ -818,16 +844,22 @@
         scatter_z(p, stream, 0, near, mate, near).wait_recv()
         scatter_z(p, stream, 0, near, z, near).wait_send()
         scatter_z(p, stream, 1, mate, z, mate).wait_send()
-        block_sum[:, columns(p)] = (
-            partial(p, z, own_quarter(p, stream))[...].astype(F32)
-            + from_rest(p, z_spot(p, stream, near))[...].astype(F32)
-            + from_rest(p, z_spot(p, stream, mate))[...].astype(F32)
-        )
+        if SCATTER_KINDS[p] == 2:
+            add_to(partial(p, z, slice(None)), from_z(p, stream, near), from_z(p, stream, mate))
+        else:
+            block_sum[:, columns(p)] = (
+                partial(p, z, own_quarter(p, stream))[...].astype(F32)
+                + from_z(p, stream, near)[...].astype(F32)
+                + from_z(p, stream, mate)[...].astype(F32)
+            )
 
         @pl.when(outer)
         def _():
             scatter_z(p, stream, 0, near, far, near).wait_recv()
-            block_sum[:, columns(p)] += from_rest(p, z_spot(p, stream, far))[...].astype(F32)
+            if SCATTER_KINDS[p] == 2:
+                add_to(partial(p, z, slice(None)), from_z(p, stream, far))
+            else:
+                block_sum[:, columns(p)] += from_z(p, stream, far)[...].astype(F32)
 
         scatter_z(p, stream, 2, far, z, far).wait_send()
 
@@ -844,7 +876,26 @@
     def scatter_stage(p, stage):
         late = SCATTER_KINDS[p]
         at_a = scatter_way(p)[0]
-        if stage == 0:
+        if late == 2:
+            if stage == 0:
+                scatter_start(p, 0)
+            elif stage == 1:
+                scatter_pass(p, 0)
+            elif stage == 2:
+                scatter_end(p, 0)
+                scatter_side(p, 0).start()
+                scatter_side(p, 1).start()
+            elif stage == 3:
+                scatter_side(p, 0).wait()
+                scatter_side(p, 1).wait()
+                add_to(partial(p, z, mine), from_b(p, 0, None))
+                add_to(partial(p, z, at_a), from_b(p, 1, None))
+                scatter_side(p, 2).start()
+            else:
+                scatter_side(p, 2).wait()
+                last = partial(p, z, mine)[...].astype(F32)
+                scatter_target(p)[...] = last + from_rest(p, 2 * chain)[...].astype(F32)
+        elif stage == 0:
             scatter_side(p, 0).start()
             scatter_side(p, 1).start()
         elif stage == 1:
@@ -990,18 +1041,18 @@
             loop(n_chunks, rest)
             key_grad = nn(prob_low[...], query)
             if h == 0:
-                gather_acc[0] = value_grad
-                gather_acc[1] = key_grad
+                gather_acc[0] = value_grad.astype(BF)
+                gather_acc[1] = key_grad.astype(BF)
             else:
-                gather_acc[0] += value_grad
-                gather_acc[1] = jnp.where(own, key_grad, gather_acc[1])
+                gather_acc[0] = jnp.where(own, value_grad, gather_acc[0].astype(F32)).astype(BF)
+                gather_acc[1] = jnp.where(own, key_grad, gather_acc[1].astype(F32)).astype(BF)
             flip[h * HEAD_DIM : (h + 1) * HEAD_DIM, :] = nn(
                 turned[h * HEAD_DIM : (h + 1) * HEAD_DIM, :], prob_low[...]
             ) * (HEAD_DIM**-0.5)
         query_low = flip[...].T.astype(BF)
-        value_low = gather_acc[0].astype(BF)
+        value_low = gather_acc[0]
         heads[0, pair // 2, :, where_pair] = query_low
-        heads[1, pair // 2, :, where_pair] = gather_acc[1].astype(BF)
+        heads[1, pair // 2, :, where_pair] = gather_acc[1]
         heads[2, pair // 2, :, where_pair] = value_low
         head_sums[0, pair] = jnp.sum(query_low.astype(F32), axis=0, keepdims=True)
         head_sums[1, pair] = jnp.sum(value_low.astype(F32), axis=0, keepdims=True)
@@ -1255,8 +1306,8 @@
         out_specs=[anywhere] * 2 + [vmem] * 5,
         scratch_shapes=[
             pltpu.VMEM((20, chain, 4) + block, BF),
-            pltpu.VMEM((PIECES, 2, chain) + block, BF),
-            pltpu.VMEM((PIECES, 2 * chain + 1) + block, BF),
+            pltpu.VMEM((PIECES, 4 * chain + 1) + block, BF),
+            pltpu.VMEM((2,) + block, BF),
             pltpu.VMEM((slots, width), BF),
             pltpu.VMEM((slots, width), BF),
             pltpu.VMEM((slots, width), BF),
@@ -1276,7 +1327,7 @@
             pltpu.VMEM((slots, slots), BF),
             pltpu.VMEM((128, slots), F32),
             pltpu.VMEM((128, slots), BF),
-            pltpu.VMEM((2, slots, 128), F32),
+            pltpu.VMEM((2, slots, 128), BF),
             pltpu.VMEM((8, 1, slots), F32),
             pltpu.VMEM((6, 8, width), F32),
             pltpu.VMEM((8, 1, TILE), F32),

time: 230 us -> 226 us (0.983); the launches traced: 228 us -> 226 us
  no operation moved by 1% of the time
where the time goes in v3:
time: 226 us
  Pallas kernels  225 us (100%)
    pallas_call x1, Pallas kernels, on_device_fused(): pl.pallas_call(functools.partial(layer_kernel, chain), out_shape=(jax.Sha...  220 us
    pallas_call x1, Pallas kernels, on_device_fused(): pl.pallas_call(finish_kernel, out_shape=(jax.ShapeDtypeStruct(tokens.shap...  4.89 us

profile of v3, /device:TPU:0, one launch (start us, length us, event | category | flops | bytes accessed | tf_op | source)
XLA Modules:
  0.0 226.1 jit_solution(2944622965353053827)
XLA Ops:
  0.7 220.3 %layer.1 = (bf16[2,320,1024]{2,1,0:T(8,128)(2,1)}, bf16[2,320,1024]{2,1,0:T(8,128)(2,1)}, f32[3,64,512]{2,1,0:T(8,128)}, f32[64,512]{1,0:T(8,128)}, f32[64,2048]...) custom-call(bf16[2,320,1024]{2,1,0:T(8,128)(2,1)} %tokens.1, bf16[2,320,1024]{2,1,0:T(8,128)(2,1)} %cotangent.1, ...), custom_call_target="tpu_custom_call" | custom-call | tf_op jit(solution)/shard_map/layer/pallas_call | solution.py:1294
  221.0 4.9 %finish.1 = (bf16[2,320,1024]{2,1,0:T(8,128)(2,1)}, f32[2,320,1024]{2,1,0:T(8,128)}, f32[1024]{0:T(1024)}, f32[1024]{0:T(1024)}, f32[3,64,512]{2,1,0:T(8,128)}, ...) custom-call(bf16[2,320,1024]{2,1,0:T(8,128)(2,1)} %get-tuple-element, ...), custom_call_target="tpu_custom_call" | custom-call | tf_op jit(solution)/shard_map/finish/pallas_call | solution.py:1362
